TPU v7x, 32 devices: a whole 2x2x4 slice. The times are simulated.
32 devices in a mesh: cache: 4 (over x, core), expert: 8 (over z, y).
Axes of the slice: x: 2, y: 2, z: 4, core: 2. Of those that a mesh axis runs over, the one named last changes fastest.
Arguments:
- queries: bfloat16 [2, 32, 2048], P(None, 'expert'), may hold values from -16 to 16
- k_cache: bfloat16 [32, 4096, 256], P('expert', 'cache'), may hold values from -6 to 6
- v_cache: bfloat16 [32, 4096, 256], P('expert', 'cache'), may hold values from -6 to 6
- lengths: int32 [32], P('expert'), may hold values from 1 to 4094
- w_out: bfloat16 [2048, 2880], P('cache'), may hold values from -0.125 to 0.125
- norm_gain: float32 [2880], replicated, may hold values from 0.25 to 1.75
- w_gate: bfloat16 [8, 2880, 1440], P('cache', 'expert'), may hold values from -0.109375 to 0.109375
- w_up: bfloat16 [8, 2880, 1440], P('cache', 'expert'), may hold values from -0.109375 to 0.109375
- w_down: bfloat16 [8, 1440, 2880], P('cache', None, 'expert'), may hold values from -0.15625 to 0.15625
- expert_ids: int32 [2, 32, 4], P(None, 'expert'), may hold values from 0 to 7, all different within a row; in each aligned block of 4 rows (0 to 3, 4 to 7, ..., all dimensions but the last counted through in order) at most 2 rows name the same one
- gate_weights: float32 [2, 32, 4], P(None, 'expert'), may hold values from 0.1 to 1
Outputs:
- mixed: bfloat16 [2, 32, 2880], P(None, 'expert')
- gate_owner: bfloat16 [8, 2880, 1440], P('expert', None, 'cache')
- up_owner: bfloat16 [8, 2880, 1440], P('expert', None, 'cache')
- down_owner: bfloat16 [8, 1440, 2880], P('expert', 'cache')
Inputs may be any that keep to these rules, and one draw needn't show every extreme that they name: `expert_ids`: in each step the 4 rows of one index of expert name one expert at most 2 times; a row names 4 different experts.
All inputs are finite; a program needn't handle non-finite values.
Results may differ from a plain program's by a relative error of at most 0.015.
Values may be sent and summed in bfloat16 or wider, within the bound.
A program may use at most 64 MiB of HBM per device.

v0:
```python
import functools
import math

import jax
import jax.numpy as jnp
from jax import lax
from jax.experimental import pallas as pl
from jax.experimental.pallas import tpu as pltpu
from jax.sharding import PartitionSpec as P

D = 2880
QH = 32
KVH = 4
HD = 64
TOP = 4

MESH = pl.DeviceIdType.MESH


def exchange_kernel(
    C, E, I, wg_hbm, wu_hbm, wd_hbm, go_hbm, uo_hbm, do_hbm,
    g_in, u_in, d_in, g_stage, u_stage, g_relay, u_relay, d_relay, g_own, u_own, d_recv, d_own,
    load_sem, send1, recv1, send2, recv2, local_sem, out_sem,
):
    c = lax.axis_index("cache")
    e = lax.axis_index("expert")
    rows = g_own.shape[1]
    width = g_own.shape[2]

    loads = [
        pltpu.make_async_copy(wd_hbm, d_in, load_sem.at[0]),
        pltpu.make_async_copy(wg_hbm, g_in, load_sem.at[1]),
        pltpu.make_async_copy(wu_hbm, u_in, load_sem.at[2]),
    ]
    for load in loads:
        load.start()

    barrier = pltpu.get_barrier_semaphore()
    for k in range(1, C):
        pl.semaphore_signal(barrier, inc=1, device_id=(lax.rem(c + k, C), e), device_id_type=MESH)
    for k in range(1, E):
        pl.semaphore_signal(barrier, inc=1, device_id=(c, lax.rem(e + k, E)), device_id_type=MESH)
    pl.semaphore_wait(barrier, C - 1 + E - 1)

    relays = (d_relay, g_relay, u_relay)
    finals = (d_recv, g_own, u_own)

    def own_part(w, target, i):
        if w == 0:
            return d_in.at[i, target]
        return (g_stage, u_stage)[w - 1].at[target, i]

    def first(w, k, i):
        target = lax.rem(c + k, C)
        return pltpu.make_async_remote_copy(
            src_ref=own_part(w, target, i),
            dst_ref=relays[w].at[c, i],
            send_sem=send1.at[w, target, i],
            recv_sem=recv1.at[w, c, i],
            device_id=(target, e),
            device_id_type=MESH,
        )

    def first_arrived(w, source, i):
        pltpu.make_async_remote_copy(
            src_ref=relays[w].at[source, i],
            dst_ref=relays[w].at[source, i],
            send_sem=send1.at[w, source, i],
            recv_sem=recv1.at[w, source, i],
            device_id=(source, e),
            device_id_type=MESH,
        ).wait_recv()

    def second_ref(w, k, i):
        source = lax.rem(c + C - k, C)
        owner = source * I + i
        part = own_part(w, c, i) if k == 0 else relays[w].at[source, i]
        return source, owner, part

    def second(w, k, i, action):
        source, owner, part = second_ref(w, k, i)

        @pl.when(owner != e)
        def _():
            copy = pltpu.make_async_remote_copy(
                src_ref=part,
                dst_ref=finals[w].at[e],
                send_sem=send2.at[w, source, i],
                recv_sem=recv2.at[w, e],
                device_id=(c, owner),
                device_id_type=MESH,
            )
            if action == "start":
                copy.start()
            else:
                copy.wait_send()

        @pl.when(owner == e)
        def _():
            copy = pltpu.make_async_copy(part, finals[w].at[e], local_sem.at[w])
            if action == "start":
                copy.start()
            else:
                copy.wait()

    order = [k for k in range(2, C)] + [1] if C > 2 else list(range(1, C))
    for w in range(3):
        loads[w].wait()
        for i in range(I):
            if w > 0:
                source = (g_in, u_in)[w - 1]
                stage = (g_stage, u_stage)[w - 1]
                for target in range(C):
                    stage[target, i] = source[i, :, target * width : (target + 1) * width]
            for k in order:
                first(w, k, i).start()
        for i in range(I):
            second(w, 0, i, "start")
    for w in range(3):
        for i in range(I):
            for k in [1] + order[:-1]:
                first_arrived(w, lax.rem(c + C - k, C), i)
                second(w, k, i, "start")
    outs = []
    for w in range(3):
        for k in range(C):
            for i in range(I):
                second(w, k, i, "wait")
        for k in range(1, E):
            source = lax.rem(e + k, E)
            pltpu.make_async_remote_copy(
                src_ref=finals[w].at[source],
                dst_ref=finals[w].at[source],
                send_sem=send2.at[w, 0, 0],
                recv_sem=recv2.at[w, source],
                device_id=(c, source),
                device_id_type=MESH,
            ).wait_recv()
        if w == 0:
            chunk = 8 * max(n for n in range(1, 16) if d_own.shape[0] % (8 * n) == 0)

            def assemble(t, carry):
                span = pl.ds(pl.multiple_of(t * chunk, chunk), chunk)
                d_own[span, :] = jnp.concatenate([d_recv[s, span, :] for s in range(E)], axis=-1)
                return carry

            lax.fori_loop(0, d_own.shape[0] // chunk, assemble, 0)
            done = pltpu.make_async_copy(d_own, do_hbm, out_sem.at[0])
        else:
            done = pltpu.make_async_copy(finals[w], (go_hbm, uo_hbm)[w - 1], out_sem.at[w])
        done.start()
        outs.append(done)
    for w in range(3):
        for i in range(I):
            for k in range(1, C):
                first(w, k, i).wait_send()
    for done in outs:
        done.wait()


def exchange(w_gate, w_up, w_down):
    C = lax.axis_size("cache")
    E = lax.axis_size("expert")
    I, rows, hidden_width = w_gate.shape
    width = hidden_width // C
    bf16 = jnp.bfloat16
    shape = jax.ShapeDtypeStruct
    any_spec = pl.BlockSpec(memory_space=pl.ANY)
    gate, up, down = pl.pallas_call(
        functools.partial(exchange_kernel, C, E, I),
        out_shape=(
            shape((E, rows, width), bf16),
            shape((E, rows, width), bf16),
            shape((width, E * rows), bf16),
        ),
        in_specs=[any_spec] * 3,
        out_specs=(any_spec,) * 3,
        scratch_shapes=[
            pltpu.VMEM((I, rows, hidden_width), bf16),
            pltpu.VMEM((I, rows, hidden_width), bf16),
            pltpu.VMEM((I, C, width, rows), bf16),
            pltpu.VMEM((C, I, rows, width), bf16),
            pltpu.VMEM((C, I, rows, width), bf16),
            pltpu.VMEM((C, I, rows, width), bf16),
            pltpu.VMEM((C, I, rows, width), bf16),
            pltpu.VMEM((C, I, width, rows), bf16),
            pltpu.VMEM((E, rows, width), bf16),
            pltpu.VMEM((E, rows, width), bf16),
            pltpu.VMEM((E, width, rows), bf16),
            pltpu.VMEM((width, E * rows), bf16),
            pltpu.SemaphoreType.DMA((3,)),
            pltpu.SemaphoreType.DMA((3, C, I)),
            pltpu.SemaphoreType.DMA((3, C, I)),
            pltpu.SemaphoreType.DMA((3, C, I)),
            pltpu.SemaphoreType.DMA((3, E)),
            pltpu.SemaphoreType.DMA((3,)),
            pltpu.SemaphoreType.DMA((3,)),
        ],
        compiler_params=pltpu.CompilerParams(
            collective_id=0, has_side_effects=True, vmem_limit_bytes=60 << 20
        ),
    )(w_gate, w_up, w_down.reshape(I, C, width, rows))
    return (
        gate.reshape(1, E * rows, width),
        up.reshape(1, E * rows, width),
        down.reshape(1, width, E * rows),
    )


def exchange_plain(w_gate, w_up, w_down):
    gate_owner, up_owner = (
        lax.all_to_all(
            lax.all_to_all(w, "cache", split_axis=2, concat_axis=0, tiled=True),
            "expert",
            split_axis=0,
            concat_axis=1,
            tiled=True,
        )
        for w in (w_gate, w_up)
    )
    down_owner = lax.all_to_all(
        lax.all_to_all(w_down, "cache", split_axis=1, concat_axis=0, tiled=True),
        "expert",
        split_axis=0,
        concat_axis=2,
        tiled=True,
    )
    return gate_owner, up_owner, down_owner


def shards(
    queries,
    k_cache,
    v_cache,
    lengths,
    w_out,
    norm_gain,
    w_gate,
    w_up,
    w_down,
    expert_ids,
    gate_weights,
):
    rows_local, hidden_local = w_gate.shape[1], w_gate.shape[2] // lax.axis_size("cache")
    fits = rows_local % 8 == 0 and hidden_local % 8 == 0 and w_gate.shape[0] * lax.axis_size("cache") == lax.axis_size("expert")
    gate_owner, up_owner, down_owner = (exchange if fits else exchange_plain)(w_gate, w_up, w_down)
    cache_count = lax.axis_size("cache")
    cache_place = lax.axis_index("cache")
    step_count = queries.shape[0]
    row_count = k_cache.shape[0]
    positions = k_cache.shape[1]
    group_size = QH // KVH
    heads = queries.reshape(step_count, row_count, KVH, group_size, HD).transpose(1, 2, 0, 3, 4)
    same = jnp.eye(KVH, dtype=jnp.float32)
    spread = heads[:, :, :, :, None, :] * same.astype(heads.dtype)[None, :, None, None, :, None]
    spread = spread.reshape(row_count, step_count * QH, KVH * HD)
    scores = jnp.einsum(
        "rnk,rpk->rnp", spread, k_cache, preferred_element_type=jnp.float32
    ) * (1.0 / math.sqrt(HD))
    position = cache_place * positions + jnp.arange(positions, dtype=jnp.int32)
    limit = lengths[:, None] + jnp.arange(step_count, dtype=jnp.int32)[None, :] + 1
    limit = jnp.broadcast_to(
        limit[:, None, :, None], (row_count, KVH, step_count, group_size)
    ).reshape(row_count, step_count * QH)
    visible = position[None, None, :] < limit[:, :, None]
    highest = jnp.max(jnp.where(visible, scores, -1e30), axis=-1)
    weights = jnp.where(visible, jnp.exp(scores - highest[..., None]), 0.0)
    mass = jnp.sum(weights, axis=-1)
    accum = jnp.einsum(
        "rnp,rpk->rnk",
        weights.astype(jnp.bfloat16),
        v_cache,
        preferred_element_type=jnp.float32,
    ).reshape(row_count, KVH, step_count, group_size, KVH, HD)
    accum = jnp.sum(accum * same[None, :, None, None, :, None], axis=4)

    def by_step(a):
        return jnp.moveaxis(a, 2, 0).reshape(step_count, row_count, -1)

    accum = by_step(accum)
    highest = by_step(highest.reshape(row_count, KVH, step_count, group_size))
    mass = by_step(mass.reshape(row_count, KVH, step_count, group_size))
    own_width = w_out.shape[0]
    gathered = lax.all_gather(jnp.concatenate((accum, highest, mass), axis=-1), "cache")
    own_heads = own_width // HD
    all_high = gathered[..., QH * HD : QH * HD + QH]
    factor = jnp.exp(all_high - jnp.max(all_high, axis=0))
    all_mass = jnp.sum(gathered[..., QH * HD + QH :] * factor, axis=0)
    own_factor = lax.dynamic_slice_in_dim(factor / all_mass, cache_place * own_heads, own_heads, 3)
    own_accum = lax.dynamic_slice_in_dim(gathered, cache_place * own_width, own_width, 3)
    own_out = jnp.sum(own_accum * jnp.repeat(own_factor, HD, axis=-1), axis=0)
    own_rows = own_out.astype(jnp.bfloat16).reshape(step_count * row_count, own_width)
    projected = jnp.dot(own_rows, w_out, preferred_element_type=jnp.float32)
    attention = jnp.sum(lax.all_gather(projected, "cache"), axis=0)
    scale = lax.rsqrt(jnp.mean(attention * attention, axis=-1, keepdims=True) + 1e-05)
    normed = (attention * scale * norm_gain).astype(jnp.bfloat16).reshape(step_count, row_count, D)
    experts_total = w_gate.shape[0] * cache_count
    capacity = max(2, (row_count * TOP + experts_total - 1) // experts_total)
    expert_range = jnp.arange(experts_total, dtype=jnp.int32)
    onehot = (expert_ids[..., None] == expert_range).astype(jnp.float32)
    chosen = jnp.sum(onehot, axis=2)
    gate_map = jnp.sum(onehot * gate_weights[..., None], axis=2)
    earlier = jnp.tril(jnp.ones((row_count, row_count), jnp.float32), -1)
    ranks = jnp.einsum("rq,sqe->sre", earlier, chosen, precision=lax.Precision.HIGHEST)
    slot_table = (ranks[..., None] == jnp.arange(capacity, dtype=jnp.float32)).astype(
        jnp.float32
    ) * chosen[..., None]
    outgoing = jnp.einsum(
        "srec,srd->escd",
        slot_table.astype(jnp.bfloat16),
        normed,
        preferred_element_type=jnp.float32,
    )
    outgoing = outgoing.astype(jnp.bfloat16).reshape(experts_total, step_count * capacity, D)
    slots = lax.all_to_all(outgoing, "expert", split_axis=0, concat_axis=0, tiled=True)
    source_count = slots.shape[0]
    item_count = slots.shape[1]
    slot_rows = slots.reshape(source_count * item_count, D)
    gate_value = jnp.dot(slot_rows, gate_owner[0], preferred_element_type=jnp.float32)
    up_value = jnp.dot(slot_rows, up_owner[0], preferred_element_type=jnp.float32)
    hidden = (jax.nn.silu(gate_value) * up_value).astype(jnp.bfloat16)
    partial_out = jnp.dot(hidden, down_owner[0], preferred_element_type=jnp.float32).reshape(
        source_count, item_count, D
    )
    expert_out = partial_out.astype(jnp.bfloat16)
    returned = lax.all_to_all(expert_out, "expert", split_axis=0, concat_axis=0, tiled=True)
    back_width = returned.shape[-1]
    returned = returned.reshape(experts_total, step_count, capacity, back_width)
    combined = jnp.einsum(
        "srec,escd->srd",
        slot_table * gate_map[..., None],
        returned.astype(jnp.float32),
        precision=lax.Precision.HIGHEST,
    )
    attention_rows = attention.reshape(step_count, row_count, D)
    combined = jnp.sum(lax.all_gather(combined, "cache"), axis=0)
    mixed = (attention_rows + combined).astype(jnp.bfloat16)
    return (mixed, gate_owner, up_owner, down_owner)


def solution(mesh):
    return jax.shard_map(
        shards,
        mesh=mesh,
        in_specs=(
            P(None, "expert", None),
            P("expert", "cache", None),
            P("expert", "cache", None),
            P("expert"),
            P("cache", None),
            P(),
            P("cache", "expert", None),
            P("cache", "expert", None),
            P("cache", None, "expert"),
            P(None, "expert", None),
            P(None, "expert", None),
        ),
        out_specs=(
            P(None, "expert", None),
            P("expert", None, "cache"),
            P("expert", None, "cache"),
            P("expert", "cache", None),
        ),
        check_vma=False,
    )
```

profile of v0, /device:TPU:0, one launch (start us, length us, event | category | flops | bytes accessed | tf_op | source)
XLA Modules:
  0.0 226.9 jit_solution(9912708471896513911)
XLA Ops:
  0.6 0.0 copy-start
  0.7 0.9 add_add_fusion
  1.6 0.1 broadcast_in_dim.11
  1.6 0.1 lt.22
  1.7 0.1 mul.104
  1.8 0.1 mul.105
  1.9 0.9 reshape.145
  2.8 0.1 mul.102
  2.9 0.2 mul.103
  3.2 3.3 %fusion.1 = (f32[4,64]{1,0:T(4,128)S(1)}, f32[4,64,1024]{2,1,0:T(8,128)}) fusion(s32[4,64]{1,0:T(4,128)S(1)} %lt.22, s32[1024]{0:T(1024)S(1)} %iota_add_fusion, bf16[4,1024,256]{2,1,0:T(8,128)(2,1)} %param.12, bf16[4,64,256]{2,1,0:T(8,128)(2,1)S(1)} %mul.103, bf16[64,256]{1,0:T(8,128)(2,1)S(1)} %mul.105), kind=kOutput, calls=%fused_computation.9 | convolution fusion | flops 135331584 | bytes 3315712 | tf_op jit(solution)/shard_map/rnk,rpk->rnp/dot_general | solution.py:257
  6.5 0.1 reshape.148
  6.6 1.6 fusion.2
  8.2 3.1 %fusion.4 = f32[4,64,256]{2,1,0:T(8,128)} fusion(bf16[4,1024,256]{2,1,0:T(8,128)(2,1)} %param.13, f32[4,64,1024]{2,1,0:T(8,128)} %get-tuple-element.35, f32[4,64]{1,0:T(4,128)S(1)} %get-tuple-element.34, s32[4,64]{1,0:T(4,128)S(1)} %lt.22, s32[1024]{0:T(1024)S(1)} %iota_add_fusion), kind=kOutput, calls=%fused_computation.12 | convolution fusion | flops 135266304 | bytes 3414016 | tf_op jit(solution)/shard_map/rnp,rpk->rnk/dot_general | solution.py:269
  11.3 0.1 reshape.149
  11.4 0.1 reshape.150
  11.5 0.1 reshape.151
  11.6 1.2 reshape.146
  12.8 0.4 multiply_reduce_fusion
  13.2 0.1 reshape.147
  13.3 0.1 concatenate.3
  13.4 7.3 %all-gather = f32[8,4,2112]{2,1,0:T(4,128)S(1)} all-gather(f32[2,4,2112]{2,1,0:T(4,128)S(1)} %concatenate.3), channel_id=2, replica_groups=mesh['cache'=4,'expert'=8] {'cache'}, dimensions={0}, use_global_device_ids=true | all-gather | bytes 337920 | tf_op jit(solution)/shard_map/all_gather | solution.py:284
  20.7 0.1 fusion.22
  20.8 0.1 constant_dynamic-slice_fusion
  20.9 0.1 dynamic-slice_divide_fusion
  21.0 0.1 broadcast_in_dim.14
  21.1 0.1 reshape.152
  21.2 0.0 copy-start.2
  21.2 0.0 copy-start.3
  21.2 0.1 multiply_reduce_fusion.2
  21.3 0.0 copy-start.1
  21.4 0.0 copy-done
  21.4 0.8 fusion.43
  22.2 6.5 %all-gather.1 = f32[32,2880]{1,0:T(8,128)S(1)} all-gather(f32[8,2880]{1,0:T(8,128)S(1)} %fusion.43), channel_id=3, replica_groups=mesh['cache'=4,'expert'=8] {'cache'}, dimensions={0}, use_global_device_ids=true | all-gather | bytes 460800 | tf_op jit(solution)/shard_map/all_gather | solution.py:294
  28.7 0.1 multiply_reduce_fusion.1
  28.9 0.1 rsqrt.12
  29.0 0.0 copy-done.2
  29.0 0.0 copy-done.3
  29.0 0.1 select_reduce_fusion
  29.1 0.2 convolution_bitcast_fusion.1
  29.3 0.0 copy-done.1
  29.3 0.3 convolution_convert_fusion.1
  29.6 0.7 copy.44
  30.3 5.8 %all-to-all-start = ((bf16[8,4,2880]{2,1,0:T(4,128)(2,1)}), bf16[8,4,2880]{2,1,0:T(4,128)(2,1)S(1)}, u32[]{:S(2)}, u32[]{:S(2)}) async-start(bf16[8,4,2880]{2,1,0:T(4,128)(2,1)} %copy.44), calls=%async_computation | async-start | bytes 376832 | tf_op jit(solution)/shard_map/all_to_all | solution.py:315
  36.2 116.9 %shard_map.138 = (bf16[8,360,360]{2,1,0:T(8,128)(2,1)}, bf16[8,360,360]{2,1,0:T(8,128)(2,1)}, bf16[360,2880]{1,0:T(8,128)(2,1)}) custom-call(bf16[2,360,1440]{2,1,0:T(8,128)(2,1)} %wg_hbm.1, bf16[2,360,1440]{2,1,0:T(8,128)(2,1)} %wu_hbm.1, bf16[2,4,360,360]{3,2,1,0:T(8,128)(2,1)} %bitcast.51), custom_call_target="tpu_custom_call" | custom-call | tf_op jit(solution)/shard_map/pallas_call | solution.py:169
  153.1 0.0 all-to-all-done
  153.1 0.1 reshape.155
  153.2 2.1 fusion.44
  155.2 3.3 %convolution_convert_fusion = bf16[32,2880]{1,0:T(8,128)(2,1)S(1)} fusion(bf16[360,2880]{1,0:T(8,128)(2,1)} %get-tuple-element.9, bf16[32,2880]{1,0:T(8,128)(2,1)S(1)} %reshape.155, bf16[2880,360]{1,0:T(8,128)(2,1)} %bitcast.46, f32[32,360]{1,0:T(8,128)S(1)} %fusion.44), kind=kOutput, calls=%fused_computation | convolution fusion | flops 132871680 | bytes 4561920 | tf_op jit(solution)/shard_map/dot_general | solution.py:322
  158.5 0.7 convert_element_type.71
  159.2 49.1 %all-to-all-start.1 = ((bf16[8,4,2880]{2,1,0:T(4,128)(2,1)}), bf16[8,4,2880]{2,1,0:T(4,128)(2,1)S(1)}, u32[]{:S(2)}, u32[]{:S(2)}) async-start(bf16[8,4,2880]{2,1,0:T(4,128)(2,1)} %convert_element_type.71), calls=%async_computation.1 | async-start | bytes 376832 | tf_op jit(solution)/shard_map/all_to_all | solution.py:326
  208.4 4.1 %copy.47 = bf16[1,2880,360]{1,2,0:T(8,128)(2,1)} copy(bf16[1,2880,360]{2,1,0:T(8,128)(2,1)} %bitcast.47) | data formatting | bytes 4147200
  212.5 4.1 %copy.46 = bf16[1,2880,360]{1,2,0:T(8,128)(2,1)} copy(bf16[1,2880,360]{2,1,0:T(8,128)(2,1)} %bitcast.49) | data formatting | bytes 4147200
  216.6 0.0 all-to-all-done.1
  216.7 0.3 convolution_bitcast_fusion
  217.0 6.1 %all-gather.2 = f32[8,4,2880]{2,1,0:T(4,128)S(1)} all-gather(f32[2,4,2880]{2,1,0:T(4,128)S(1)} %convolution_bitcast_fusion), channel_id=4, replica_groups=mesh['cache'=4,'expert'=8] {'cache'}, dimensions={0}, use_global_device_ids=true | all-gather | bytes 460800 | tf_op jit(solution)/shard_map/all_gather | solution.py:336
  223.1 0.1 reduce_sum.89
  223.2 0.6 add_convert_fusion
  223.8 3.1 %copy.51 = bf16[1,360,2880]{2,1,0:T(8,128)(2,1)} copy(bf16[1,360,2880]{2,1,0:T(8,128)(2,1)} %bitcast.50) | data formatting | bytes 4147200
  (14 shorter events, 0.2 us)
Async XLA Ops:
  0.6 20.7 %copy-start = (bf16[512,2880]{0,1:T(8,128)(2,1)S(1)}, bf16[512,2880]{0,1:T(8,128)(2,1)}, u32[]{:S(2)}) copy-start(bf16[512,2880]{0,1:T(8,128)(2,1)} %param.15) | copy-start | bytes 8847364
  21.2 7.8 %copy-start.2 = (f32[2,4,4]{2,1,0:T(4,128)S(1)}, f32[2,4,4]{2,1,0:T(4,128)}, u32[]{:S(2)}) copy-start(f32[2,4,4]{2,1,0:T(4,128)} %param.21) | copy-start | bytes 388
  21.2 7.8 %copy-start.3 = (s32[2,4,4]{2,1,0:T(4,128)S(1)}, s32[2,4,4]{2,1,0:T(4,128)}, u32[]{:S(2)}) copy-start(s32[2,4,4]{2,1,0:T(4,128)} %param.20) | copy-start | bytes 388
  21.3 8.0 %copy-start.1 = (f32[2880]{0:T(1024)S(1)}, f32[2880]{0:T(1024)}, u32[]{:S(2)}) copy-start(f32[2880]{0:T(1024)} %param.16) | copy-start | bytes 34564
  30.3 122.7 %all-to-all-start = ((bf16[8,4,2880]{2,1,0:T(4,128)(2,1)}), bf16[8,4,2880]{2,1,0:T(4,128)(2,1)S(1)}, u32[]{:S(2)}, u32[]{:S(2)}) async-start(bf16[8,4,2880]{2,1,0:T(4,128)(2,1)} %copy.44), calls=%async_computation | async-start | bytes 376832 | tf_op jit(solution)/shard_map/all_to_all | solution.py:315
  159.2 57.4 %all-to-all-start.1 = ((bf16[8,4,2880]{2,1,0:T(4,128)(2,1)}), bf16[8,4,2880]{2,1,0:T(4,128)(2,1)S(1)}, u32[]{:S(2)}, u32[]{:S(2)}) async-start(bf16[8,4,2880]{2,1,0:T(4,128)(2,1)} %convert_element_type.71), calls=%async_computation.1 | async-start | bytes 376832 | tf_op jit(solution)/shard_map/all_to_all | solution.py:326
where the time goes:
time: 228 us; the launch traced here: 227 us
  Pallas kernels  117 us (51%)
  starting transfers between devices  55 us (24%)
  blocking collectives  19.9 us (9%)
  local copies, waits for them, and re-layouts  16.7 us (7%)
  matrix products  13.4 us (6%)
  other arithmetic  4.19 us (2%)
    pallas_call x1, Pallas kernels, exchange(): pl.pallas_call(functools.partial(exchange_kernel, C, E, I), out_shape=(sh...  117 us
    all_to_all x1, starting transfers between devices, shards(): lax.all_to_all(expert_out, 'expert', split_axis=0, concat_axis=0, tiled=T...  49.1 us
    unnamed x11, local copies, waits for them, and re-layouts  11.4 us
    all_gather x1, blocking collectives, shards(): lax.all_gather(jnp.concatenate((accum, highest, mass), axis=-1), 'cache')  7.3 us
    all_gather x1, blocking collectives, shards(): attention = jnp.sum(lax.all_gather(projected, 'cache'), axis=0)  6.49 us
    all_gather x1, blocking collectives, shards(): combined = jnp.sum(lax.all_gather(combined, 'cache'), axis=0)  6.1 us
    all_to_all x1, starting transfers between devices, shards(): lax.all_to_all(outgoing, 'expert', split_axis=0, concat_axis=0, tiled=True)  5.83 us
  transfers between devices with their start and end apart: 2, of which 0 were waited for; matrix products, arithmetic and copies ran while one was open for 4% of the time, Pallas kernels for 52%

commit v1 on v0

v1 whole, which is shorter than its diff:
```python
import functools
import math

import jax
import jax.numpy as jnp
from jax import lax
from jax.experimental import pallas as pl
from jax.experimental.pallas import tpu as pltpu
from jax.sharding import PartitionSpec as P

D = 2880
QH = 32
KVH = 4
HD = 64
TOP = 4
NEAR = 2

MESH = pl.DeviceIdType.MESH
F32 = jnp.float32
BF16 = jnp.bfloat16


def dot_nt(a, b):
    return lax.dot_general(a, b, (((1,), (1,)), ((), ())), preferred_element_type=F32)


def dot_nn(a, b):
    return jnp.dot(a, b, preferred_element_type=F32)


def iota(shape, axis):
    return lax.broadcasted_iota(jnp.int32, shape, axis)


def whole_kernel(
    C, E, I, S, R, cap,
    lengths, ids, gates, q_ref, gain_ref, k_hbm, v_hbm, wo_hbm, wg_hbm, wu_hbm, wd_hbm,
    g_own, u_own, d_own, mixed_ref,
    g_in, u_in, d_in, g_stage, u_stage, relay_g, relay_u, relay_d, fin_g, fin_u, fin_d,
    k_in, v_in, wo_in, q_f32, part_out, part_in, proj, normed, out_slots, in_slots, slots_bf, slots_all,
    rows_x, hid_out, hid_in, back_out, back_in, comb,
    load_sem, sx, r1, sd, sr, rf, loc, s_part, r_part, s_proj, r_proj, s_disp, r_disp, s_slot, r_slot,
    s_hid, r_hid, s_back, r_back, s_comb, r_comb,
):
    c = lax.axis_index("cache")
    e = lax.axis_index("expert")
    x = c // NEAR
    k = lax.rem(c, NEAR)
    O = C - NEAR
    width = g_own.shape[0]
    rows = fin_g.shape[2]
    group = QH // KVH
    per_row = group * S
    heads_rows = KVH * per_row
    items = S * cap
    total = S * R
    chunk = out_slots.shape[1] * 2
    half = chunk // 2
    d_model = E * rows

    loads = []
    for i in range(I):
        loads.append(pltpu.make_async_copy(wg_hbm.at[i], g_in.at[i], load_sem.at[0, i]))
    loads.append(pltpu.make_async_copy(k_hbm, k_in, load_sem.at[3, 0]))
    loads.append(pltpu.make_async_copy(v_hbm, v_in, load_sem.at[3, 1]))
    for i in range(I):
        loads.append(pltpu.make_async_copy(wu_hbm.at[i], u_in.at[i], load_sem.at[1, i]))
    loads.append(pltpu.make_async_copy(wd_hbm, d_in, load_sem.at[2, 0]))
    loads.append(pltpu.make_async_copy(wo_hbm, wo_in, load_sem.at[2, 1]))
    for load in loads:
        load.start()
    load_g, load_k, load_v = loads[:I], loads[I], loads[I + 1]
    load_u, load_d, load_wo = loads[I + 2 : 2 * I + 2], loads[2 * I + 2], loads[2 * I + 3]

    barrier = pltpu.get_barrier_semaphore()
    me = c * E + e
    for n in range(1, C * E):
        other = lax.rem(me + n, C * E)
        pl.semaphore_signal(barrier, inc=1, device_id=(other // E, lax.rem(other, E)), device_id_type=MESH)
    pl.semaphore_wait(barrier, C * E - 1)

    relays = (relay_g, relay_u, relay_d)
    finals = (fin_g, fin_u, fin_d)

    def remote(src, dst, send, recv, tc, te):
        return pltpu.make_async_remote_copy(
            src_ref=src, dst_ref=dst, send_sem=send, recv_sem=recv, device_id=(tc, te), device_id_type=MESH
        )

    def block(w, i, target):
        return (g_stage, u_stage, d_in)[w].at[i, target]

    def far(o):
        return lax.rem(x * NEAR + NEAR + o, C)

    def direct(w, i, kd, action):
        target = x * NEAR + kd
        owner = c * I + i
        own = (owner == e) & (k == kd)

        @pl.when(own)
        def _():
            if action == "start":
                pltpu.make_async_copy(block(w, i, target), finals[w].at[e], loc.at[w]).start()

        @pl.when(jnp.logical_not(own))
        def _():
            copy = remote(block(w, i, target), finals[w].at[e], sd.at[w, i, kd], rf.at[w, e], target, owner)
            copy.start() if action == "start" else copy.wait_send()

    def hop(w, i, o, action):
        target = far(o)
        owner = c * I + i
        place = lax.rem(c - (target // NEAR) * NEAR - NEAR + 2 * C, C)

        @pl.when(owner == e)
        def _():
            copy = remote(block(w, i, target), finals[w].at[e], sx.at[w, i, o], rf.at[w, e], target, e)
            copy.start() if action == "start" else copy.wait_send()

        @pl.when(owner != e)
        def _():
            copy = remote(block(w, i, target), relays[w].at[place, i], sx.at[w, i, o], r1.at[w, place, i], target, e)
            copy.start() if action == "start" else copy.wait_send()

    def pass_on(w, o, i, action):
        owner = far(o) * I + i

        @pl.when(owner != e)
        def _():
            part = relays[w].at[o, i]
            copy = remote(part, finals[w].at[e], sr.at[w, o, i], rf.at[w, e], c, owner)
            if action == "start":
                remote(part, part, sr.at[w, o, i], r1.at[w, o, i], c, owner).wait_recv()
                copy.start()
            else:
                copy.wait_send()

    def arrived(w, s):
        own = (c == e // I) & (e == s)

        @pl.when(own)
        def _():
            pltpu.make_async_copy(finals[w].at[s], finals[w].at[s], loc.at[w]).wait()

        @pl.when(jnp.logical_not(own))
        def _():
            remote(finals[w].at[s], finals[w].at[s], sd.at[w, 0, 0], rf.at[w, s], c, s).wait_recv()

    def stage(w, i):
        source, target = (g_in, u_in)[w], (g_stage, u_stage)[w]
        for t in range(C):
            target[i, t] = source[i, :, t * width : (t + 1) * width].T

    def put_together(w):
        own = (g_own, u_own, d_own)[w]
        for s in range(E):
            arrived(w, s)
            own[:, s * rows : (s + 1) * rows] = finals[w][s]

    for i in range(I):
        load_g[i].wait()
        stage(0, i)
        for o in range(O):
            hop(0, i, o, "start")
        for kd in range(NEAR):
            direct(0, i, kd, "start")

    for s in range(S):
        q_f32[s * R : (s + 1) * R, :] = q_ref[s].astype(F32)
    lane_q = iota((heads_rows, QH * HD), 1)
    row_q = iota((heads_rows, QH * HD), 0)
    head_of_row = (row_q // per_row) * group + lax.rem(row_q, per_row) // S
    mine = (lane_q // HD) == head_of_row
    step_q = lax.rem(row_q, S)
    fold_l = iota((QH * HD, KVH * HD), 0)
    fold_m = iota((QH * HD, KVH * HD), 1)
    fold = ((lax.rem(fold_l, HD) == lax.rem(fold_m, HD)) & (fold_l // (group * HD) == fold_m // HD)).astype(F32).astype(BF16)
    load_k.wait()
    load_v.wait()
    positions = k_in.shape[1]
    place_of = c * positions + iota((heads_rows, positions), 1)
    step_p = lax.rem(iota((heads_rows, positions), 0), S)
    lane_t = iota((per_row, 128), 1)
    for r in range(R):
        rows_q = q_f32[r : r + 1, :]
        spread = jnp.broadcast_to(rows_q, (heads_rows, QH * HD))
        for s in range(1, S):
            spread = jnp.where(step_q == s, jnp.broadcast_to(q_f32[s * R + r : s * R + r + 1, :], spread.shape), spread)
        spread = jnp.where(mine, spread, 0.0).astype(BF16)
        spread = dot_nn(spread, fold).astype(BF16)
        score = dot_nt(spread, k_in[r]) * (1.0 / math.sqrt(HD))
        visible = place_of < lengths[r] + step_p + 1
        highest = jnp.max(jnp.where(visible, score, -1e30), axis=1, keepdims=True)
        weight = jnp.where(visible, jnp.exp(score - highest), 0.0)
        mass = jnp.sum(weight, axis=1, keepdims=True)
        accum = dot_nn(weight.astype(BF16), v_in[r])
        for h in range(KVH):
            span = slice(h * per_row, (h + 1) * per_row)
            base = (h * HD // 128) * 128
            piece = accum[span, base : base + 128]
            if h * HD % 128:
                piece = pltpu.roll(piece, 128 - HD, 1)
            piece = jnp.where(lane_t < HD, piece, jnp.where(lane_t < HD + 32, highest[span], mass[span]))
            part_out[h, r * per_row : (r + 1) * per_row, :] = piece

    def part(n, action):
        target = lax.rem(c + n, C)
        if action == "recv":
            remote(part_in.at[target], part_in.at[target], s_part.at[target], r_part.at[target], target, e).wait_recv()
            return
        copy = remote(part_out.at[target], part_in.at[c], s_part.at[target], r_part.at[c], target, e)
        copy.start() if action == "start" else copy.wait_send()

    for n in range(1, C):
        part(n, "start")
    part_in[c] = part_out[c]

    for i in range(I):
        load_u[i].wait()
        stage(1, i)
        for o in range(O):
            hop(1, i, o, "start")
        for o in range(O):
            pass_on(0, o, i, "start")
        for kd in range(NEAR):
            direct(1, i, kd, "start")

    def table(shape, row_axis):
        row = iota(shape, row_axis)
        slot = iota(shape, 1 - row_axis)
        expert = slot // (2 * items)
        inside = lax.rem(slot, items)
        chosen = jnp.zeros(shape, F32)
        weight = jnp.zeros(shape, F32)
        for s in range(S):
            for r in range(R):
                for t in range(TOP):
                    hit = (row == s * R + r) & (expert == ids[s, r, t])
                    chosen = jnp.where(hit, 1.0, chosen)
                    weight = jnp.where(hit, gates[s, r, t], weight)
        rank = jnp.zeros(shape, F32)
        place = lax.rem(row, R)
        for n in range(1, R):
            rank = rank + jnp.where(place >= n, pltpu.roll(chosen, n, row_axis), 0.0)
        fit = (row < total) & (inside // cap == row // R) & (rank == lax.rem(inside, cap).astype(F32))
        chosen = jnp.where(fit, chosen, 0.0)
        return chosen, weight * chosen

    send_table, _ = table((E * 2 * items, 128), 1)
    _, gate_table = table((total, 128), 0)

    for n in range(1, C):
        part(n, "recv")
    tall = R * per_row
    top = part_in[0][:, HD : HD + 1]
    for s in range(1, C):
        top = jnp.maximum(top, part_in[s][:, HD : HD + 1])
    number = jnp.zeros((tall, 128), F32)
    mass = jnp.zeros((tall, 1), F32)
    for s in range(C):
        one = part_in[s]
        factor = jnp.exp(one[:, HD : HD + 1] - top)
        number = number + one * factor
        mass = mass + one[:, HD + 32 : HD + 33] * factor
    number = number / mass
    lane_h = iota((tall, 128), 1)
    number = jnp.where(lane_h < HD, number, pltpu.roll(number, HD, 1))
    number = jnp.concatenate([number] * (group * HD // 128), axis=1)
    lane_w = iota(number.shape, 1)
    row_w = iota(number.shape, 0)
    number = jnp.where(lane_w // HD == lax.rem(row_w, per_row) // S, number, 0.0).astype(BF16)
    row_s = iota((total, tall), 0)
    col_s = iota((total, tall), 1)
    gather = ((col_s // per_row == lax.rem(row_s, R)) & (lax.rem(col_s, S) == row_s // R)).astype(F32).astype(BF16)
    heads_out = dot_nn(gather, number).astype(BF16)
    load_wo.wait()
    proj[c] = dot_nt(heads_out, wo_in[...])

    def gather_cache(buffer, send, recv, n, action):
        target = lax.rem(c + n, C)
        if action == "recv":
            remote(buffer.at[target], buffer.at[target], send.at[target], recv.at[target], target, e).wait_recv()
            return
        copy = remote(buffer.at[c], buffer.at[c], send.at[target], recv.at[c], target, e)
        copy.start() if action == "start" else copy.wait_send()

    for n in range(1, C):
        gather_cache(proj, s_proj, r_proj, n, "start")

    load_d.wait()
    for i in range(I):
        for o in range(O):
            hop(2, i, o, "start")
    for i in range(I):
        for o in range(O):
            pass_on(1, o, i, "start")
    for n in range(1, C):
        gather_cache(proj, s_proj, r_proj, n, "recv")
    attention = proj[0]
    for s in range(1, C):
        attention = attention + proj[s]
    scale = lax.rsqrt(jnp.sum(attention * attention, axis=1, keepdims=True) * (1.0 / d_model) + 1e-05)
    normed[:, d_model:] = jnp.zeros((total, C * chunk - d_model), F32)
    normed[:, :d_model] = (attention * scale * gain_ref[...]).astype(BF16).astype(F32)
    own_chunk = normed[:, pl.ds(pl.multiple_of(c * chunk, 128), chunk)]
    placed = dot_nn(send_table[:, :total], own_chunk)
    upper = lax.rem(iota((E * 2 * items, half), 0), 2 * items) < items
    out_slots[...] = jnp.where(upper, placed[:, :half], placed[:, half:])
    step8 = 2 * items

    def at_expert(buffer, index):
        return buffer.at[pl.ds(pl.multiple_of(index * step8, step8), step8)]

    def spread_expert(out, back, send, recv, n, action):
        target = lax.rem(e + n, E)
        if action == "recv":
            spot = at_expert(back, target)
            remote(spot, spot, send.at[target], recv.at[target], c, target).wait_recv()
            return
        copy = remote(at_expert(out, target), at_expert(back, e), send.at[target], recv.at[e], c, target)
        copy.start() if action == "start" else copy.wait_send()

    for n in range(1, E):
        spread_expert(out_slots, in_slots, s_disp, r_disp, n, "start")
    in_slots[pl.ds(pl.multiple_of(e * step8, step8), step8), :] = out_slots[pl.ds(pl.multiple_of(e * step8, step8), step8), :]

    direct(2, 0, 0, "start")
    direct(2, 0, 1, "start")
    for i in range(I):
        for o in range(O):
            pass_on(2, o, i, "start")
    for n in range(1, E):
        spread_expert(out_slots, in_slots, s_disp, r_disp, n, "recv")
    slots_all[c] = in_slots[...].astype(BF16)
    for n in range(1, C):
        gather_cache(slots_all, s_slot, r_slot, n, "start")
    for n in range(1, C):
        gather_cache(slots_all, s_slot, r_slot, n, "recv")
    count = E * items
    row_t = iota((count, 2 * count), 0)
    col_t = iota((count, 2 * count), 1)
    base = (row_t // items) * step8 + lax.rem(row_t, items)
    take_low = (col_t == base).astype(F32).astype(BF16)
    take_high = (col_t == base + items).astype(F32).astype(BF16)
    for s in range(C):
        rows_x[:, s * chunk : s * chunk + half] = dot_nn(take_low, slots_all[s]).astype(BF16)
        rows_x[:, s * chunk + half : (s + 1) * chunk] = dot_nn(take_high, slots_all[s]).astype(BF16)

    put_together(0)
    gate_value = dot_nt(rows_x[:, :d_model], g_own[...])
    put_together(1)
    up_value = dot_nt(rows_x[:, :d_model], u_own[...])
    hid_out[...] = (gate_value * jax.nn.sigmoid(gate_value) * up_value).astype(BF16)

    column = e // I
    inner = lax.rem(e, I)

    def hidden(n, action):
        target = lax.rem(e + n, E)
        own = (column == c) & (target == e)

        @pl.when(jnp.logical_not(own))
        def _():
            copy = remote(hid_out, hid_in.at[inner, c], s_hid.at[target], r_hid.at[inner, c], column, target)
            copy.start() if action == "start" else copy.wait_send()

        if n == 0 and action == "start":

            @pl.when(own)
            def _():
                hid_in[inner, c] = hid_out[...]

    for n in range(E):
        hidden(n, "start")
    for i in range(1, I):
        for kd in range(NEAR):
            direct(2, i, kd, "start")
    down = []
    for i in range(I):
        value = jnp.zeros((count, rows), F32)
        for s in range(C):
            @pl.when(jnp.logical_not((s == c) & (e == c * I + i)))
            def _():
                remote(hid_in.at[i, s], hid_in.at[i, s], s_hid.at[0], r_hid.at[i, s], s, e).wait_recv()
            value = value + dot_nn(hid_in[i, s], d_in[i, s])
        down.append(value.astype(BF16))
    row_b = iota((I * count, count), 0)
    col_b = iota((I * count, count), 1)
    back = jnp.zeros((I * count, rows), F32)
    for i in range(I):
        pick = (col_b == (row_b // (I * items)) * items + lax.rem(row_b, I * items) - i * items) & (
            lax.rem(row_b, I * items) // items == i
        )
        back = back + dot_nn(pick.astype(F32).astype(BF16), down[i])
    back_out[...] = back
    for n in range(1, E):
        spread_expert(back_out, back_in, s_back, r_back, n, "start")
    back_in[pl.ds(pl.multiple_of(e * step8, step8), step8), :] = back_out[pl.ds(pl.multiple_of(e * step8, step8), step8), :]
    turned = pltpu.roll(gate_table, lax.rem(128 - c * (I * 2 * items), 128), 1)
    for n in range(1, E):
        spread_expert(back_out, back_in, s_back, r_back, n, "recv")
    for s in range(E):
        value = jnp.zeros((total, rows), F32)
        for i in range(I):
            for j in range(items):
                line = back_in[s * step8 + i * items + j : s * step8 + i * items + j + 1, :]
                lane = i * 2 * items + j
                value = value + turned[:, lane : lane + 1] * line
        comb[c, s] = value
    for n in range(1, C):
        gather_cache(comb, s_comb, r_comb, n, "start")
    put_together(2)
    for n in range(1, C):
        gather_cache(comb, s_comb, r_comb, n, "recv")
    pieces = []
    for s in range(E):
        value = comb[0, s]
        for m in range(1, C):
            value = value + comb[m, s]
        pieces.append(value)
    mixed_ref[...] = attention + jnp.concatenate(pieces, axis=1)

    for w in range(3):
        for i in range(I):
            for o in range(O):
                hop(w, i, o, "send")
                pass_on(w, o, i, "send")
            for kd in range(NEAR):
                direct(w, i, kd, "send")
    for n in range(1, C):
        part(n, "send")
        gather_cache(proj, s_proj, r_proj, n, "send")
        gather_cache(slots_all, s_slot, r_slot, n, "send")
        gather_cache(comb, s_comb, r_comb, n, "send")
    for n in range(1, E):
        spread_expert(out_slots, in_slots, s_disp, r_disp, n, "send")
        spread_expert(back_out, back_in, s_back, r_back, n, "send")
    for n in range(E):
        hidden(n, "send")


def store_kernel(S, R, g_ref, u_ref, d_ref, mixed_ref, go_hbm, uo_hbm, do_hbm, mo_ref, sems):
    copies = [
        pltpu.make_async_copy(source, target, sems.at[n])
        for n, (source, target) in enumerate(((g_ref, go_hbm), (u_ref, uo_hbm), (d_ref, do_hbm)))
    ]
    for copy in copies:
        copy.start()
    for s in range(S):
        mo_ref[s] = mixed_ref[s * R : (s + 1) * R, :].astype(BF16)
    for copy in copies:
        copy.wait()


def whole_shards(
    queries, k_cache, v_cache, lengths, w_out, norm_gain, w_gate, w_up, w_down, expert_ids, gate_weights
):
    C = lax.axis_size("cache")
    E = lax.axis_size("expert")
    I, rows, hidden_width = w_gate.shape
    width = hidden_width // C
    S, R = queries.shape[0], queries.shape[1]
    positions = k_cache.shape[1]
    d_model = E * rows
    cap = 2
    items = S * cap
    O = C - NEAR
    chunk = 256 * (-(-d_model // (256 * C)))
    shape = jax.ShapeDtypeStruct
    any_spec = pl.BlockSpec(memory_space=pl.ANY)
    vmem = pl.BlockSpec(memory_space=pltpu.VMEM)
    smem = pl.BlockSpec(memory_space=pltpu.SMEM)
    V = pltpu.VMEM
    sem = pltpu.SemaphoreType.DMA
    per_row = QH // KVH * S
    gate, up, down, mixed = pl.pallas_call(
        functools.partial(whole_kernel, C, E, I, S, R, cap),
        out_shape=(
            pltpu.VMEM((width, d_model), BF16),
            pltpu.VMEM((width, d_model), BF16),
            pltpu.VMEM((width, d_model), BF16),
            pltpu.VMEM((S * R, d_model), F32),
        ),
        in_specs=[smem, smem, smem, vmem, vmem] + [any_spec] * 6,
        out_specs=(vmem,) * 4,
        scratch_shapes=[
            V((I, rows, hidden_width), BF16),
            V((I, rows, hidden_width), BF16),
            V((I, C, width, rows), BF16),
            V((I, C, width, rows), BF16),
            V((I, C, width, rows), BF16),
            V((O, I, width, rows), BF16),
            V((O, I, width, rows), BF16),
            V((O, I, width, rows), BF16),
            V((E, width, rows), BF16),
            V((E, width, rows), BF16),
            V((E, width, rows), BF16),
            V(k_cache.shape, BF16),
            V(v_cache.shape, BF16),
            V((d_model, w_out.shape[0]), BF16),
            V((S * R, QH * HD), F32),
            V((C, R * per_row, 128), F32),
            V((C, R * per_row, 128), F32),
            V((C, S * R, d_model), F32),
            V((S * R, C * chunk), F32),
            V((E * 2 * items, chunk // 2), F32),
            V((E * 2 * items, chunk // 2), F32),
            V((8, 128), BF16),
            V((C, E * 2 * items, chunk // 2), BF16),
            V((E * items, C * chunk), BF16),
            V((E * items, width), BF16),
            V((I, C, E * items, width), BF16),
            V((I * E * items, rows), F32),
            V((I * E * items, rows), F32),
            V((C, E, S * R, rows), F32),
            sem((4, 2)),
            sem((3, I, O)),
            sem((3, O, I)),
            sem((3, I, NEAR)),
            sem((3, O, I)),
            sem((3, E)),
            sem((3,)),
            sem((C,)),
            sem((C,)),
            sem((C,)),
            sem((C,)),
            sem((E,)),
            sem((E,)),
            sem((C,)),
            sem((C,)),
            sem((E,)),
            sem((I, C)),
            sem((E,)),
            sem((E,)),
            sem((C,)),
            sem((C,)),
        ],
        compiler_params=pltpu.CompilerParams(
            collective_id=0, has_side_effects=True, vmem_limit_bytes=54 << 20
        ),
    )(
        lengths,
        expert_ids,
        gate_weights,
        queries,
        norm_gain.reshape(1, d_model),
        k_cache,
        v_cache,
        w_out.T,
        w_gate,
        w_up,
        w_down.reshape(I, C, width, rows),
    )
    gate, up, down, mixed = (pltpu.with_memory_space_constraint(a, pltpu.VMEM) for a in (gate, up, down, mixed))
    gate, up, down, mixed = pl.pallas_call(
        functools.partial(store_kernel, S, R),
        out_shape=(
            shape((width, d_model), BF16),
            shape((width, d_model), BF16),
            shape((width, d_model), BF16),
            shape((S, R, d_model), BF16),
        ),
        in_specs=[vmem] * 4,
        out_specs=(any_spec,) * 3 + (vmem,),
        scratch_shapes=[sem((3,))],
        compiler_params=pltpu.CompilerParams(vmem_limit_bytes=2 << 20),
    )(gate, up, down, mixed)
    return (
        mixed,
        gate.T.reshape(1, d_model, width),
        up.T.reshape(1, d_model, width),
        down.reshape(1, width, d_model),
    )


def exchange_plain(w_gate, w_up, w_down):
    gate_owner, up_owner = (
        lax.all_to_all(
            lax.all_to_all(w, "cache", split_axis=2, concat_axis=0, tiled=True),
            "expert",
            split_axis=0,
            concat_axis=1,
            tiled=True,
        )
        for w in (w_gate, w_up)
    )
    down_owner = lax.all_to_all(
        lax.all_to_all(w_down, "cache", split_axis=1, concat_axis=0, tiled=True),
        "expert",
        split_axis=0,
        concat_axis=2,
        tiled=True,
    )
    return gate_owner, up_owner, down_owner


def plain_shards(
    queries,
    k_cache,
    v_cache,
    lengths,
    w_out,
    norm_gain,
    w_gate,
    w_up,
    w_down,
    expert_ids,
    gate_weights,
):
    gate_owner, up_owner, down_owner = exchange_plain(w_gate, w_up, w_down)
    cache_count = lax.axis_size("cache")
    cache_place = lax.axis_index("cache")
    step_count = queries.shape[0]
    row_count = k_cache.shape[0]
    positions = k_cache.shape[1]
    group_size = QH // KVH
    heads = queries.reshape(step_count, row_count, KVH, group_size, HD).transpose(1, 2, 0, 3, 4)
    same = jnp.eye(KVH, dtype=jnp.float32)
    spread = heads[:, :, :, :, None, :] * same.astype(heads.dtype)[None, :, None, None, :, None]
    spread = spread.reshape(row_count, step_count * QH, KVH * HD)
    scores = jnp.einsum(
        "rnk,rpk->rnp", spread, k_cache, preferred_element_type=jnp.float32
    ) * (1.0 / math.sqrt(HD))
    position = cache_place * positions + jnp.arange(positions, dtype=jnp.int32)
    limit = lengths[:, None] + jnp.arange(step_count, dtype=jnp.int32)[None, :] + 1
    limit = jnp.broadcast_to(
        limit[:, None, :, None], (row_count, KVH, step_count, group_size)
    ).reshape(row_count, step_count * QH)
    visible = position[None, None, :] < limit[:, :, None]
    highest = jnp.max(jnp.where(visible, scores, -1e30), axis=-1)
    weights = jnp.where(visible, jnp.exp(scores - highest[..., None]), 0.0)
    mass = jnp.sum(weights, axis=-1)
    accum = jnp.einsum(
        "rnp,rpk->rnk",
        weights.astype(jnp.bfloat16),
        v_cache,
        preferred_element_type=jnp.float32,
    ).reshape(row_count, KVH, step_count, group_size, KVH, HD)
    accum = jnp.sum(accum * same[None, :, None, None, :, None], axis=4)

    def by_step(a):
        return jnp.moveaxis(a, 2, 0).reshape(step_count, row_count, -1)

    accum = by_step(accum)
    highest = by_step(highest.reshape(row_count, KVH, step_count, group_size))
    mass = by_step(mass.reshape(row_count, KVH, step_count, group_size))
    own_width = w_out.shape[0]
    gathered = lax.all_gather(jnp.concatenate((accum, highest, mass), axis=-1), "cache")
    own_heads = own_width // HD
    all_high = gathered[..., QH * HD : QH * HD + QH]
    factor = jnp.exp(all_high - jnp.max(all_high, axis=0))
    all_mass = jnp.sum(gathered[..., QH * HD + QH :] * factor, axis=0)
    own_factor = lax.dynamic_slice_in_dim(factor / all_mass, cache_place * own_heads, own_heads, 3)
    own_accum = lax.dynamic_slice_in_dim(gathered, cache_place * own_width, own_width, 3)
    own_out = jnp.sum(own_accum * jnp.repeat(own_factor, HD, axis=-1), axis=0)
    own_rows = own_out.astype(jnp.bfloat16).reshape(step_count * row_count, own_width)
    projected = jnp.dot(own_rows, w_out, preferred_element_type=jnp.float32)
    attention = jnp.sum(lax.all_gather(projected, "cache"), axis=0)
    scale = lax.rsqrt(jnp.mean(attention * attention, axis=-1, keepdims=True) + 1e-05)
    normed = (attention * scale * norm_gain).astype(jnp.bfloat16).reshape(step_count, row_count, D)
    experts_total = w_gate.shape[0] * cache_count
    capacity = max(2, (row_count * TOP + experts_total - 1) // experts_total)
    expert_range = jnp.arange(experts_total, dtype=jnp.int32)
    onehot = (expert_ids[..., None] == expert_range).astype(jnp.float32)
    chosen = jnp.sum(onehot, axis=2)
    gate_map = jnp.sum(onehot * gate_weights[..., None], axis=2)
    earlier = jnp.tril(jnp.ones((row_count, row_count), jnp.float32), -1)
    ranks = jnp.einsum("rq,sqe->sre", earlier, chosen, precision=lax.Precision.HIGHEST)
    slot_table = (ranks[..., None] == jnp.arange(capacity, dtype=jnp.float32)).astype(
        jnp.float32
    ) * chosen[..., None]
    outgoing = jnp.einsum(
        "srec,srd->escd",
        slot_table.astype(jnp.bfloat16),
        normed,
        preferred_element_type=jnp.float32,
    )
    outgoing = outgoing.astype(jnp.bfloat16).reshape(experts_total, step_count * capacity, D)
    slots = lax.all_to_all(outgoing, "expert", split_axis=0, concat_axis=0, tiled=True)
    source_count = slots.shape[0]
    item_count = slots.shape[1]
    slot_rows = slots.reshape(source_count * item_count, D)
    gate_value = jnp.dot(slot_rows, gate_owner[0], preferred_element_type=jnp.float32)
    up_value = jnp.dot(slot_rows, up_owner[0], preferred_element_type=jnp.float32)
    hidden = (jax.nn.silu(gate_value) * up_value).astype(jnp.bfloat16)
    partial_out = jnp.dot(hidden, down_owner[0], preferred_element_type=jnp.float32).reshape(
        source_count, item_count, D
    )
    expert_out = partial_out.astype(jnp.bfloat16)
    returned = lax.all_to_all(expert_out, "expert", split_axis=0, concat_axis=0, tiled=True)
    back_width = returned.shape[-1]
    returned = returned.reshape(experts_total, step_count, capacity, back_width)
    combined = jnp.einsum(
        "srec,escd->srd",
        slot_table * gate_map[..., None],
        returned.astype(jnp.float32),
        precision=lax.Precision.HIGHEST,
    )
    attention_rows = attention.reshape(step_count, row_count, D)
    combined = jnp.sum(lax.all_gather(combined, "cache"), axis=0)
    mixed = (attention_rows + combined).astype(jnp.bfloat16)
    return (mixed, gate_owner, up_owner, down_owner)


def shards(*args):
    queries, w_out, w_gate = args[0], args[4], args[6]
    C, E = lax.axis_size("cache"), lax.axis_size("expert")
    I, rows, hidden_width = w_gate.shape
    fits = (
        C % NEAR == 0
        and C > NEAR
        and C == KVH
        and I * C == E
        and rows % 8 == 0
        and hidden_width % (8 * C) == 0
        and w_out.shape[0] * C == QH * HD
        and queries.shape[0] * queries.shape[1] == 8
        and I * queries.shape[0] * 2 == 8
        and 2 * queries.shape[0] * 2 == 8
        and queries.shape[1] * TOP <= 2 * E
    )
    return (whole_shards if fits else plain_shards)(*args)


def solution(mesh):
    return jax.shard_map(
        shards,
        mesh=mesh,
        in_specs=(
            P(None, "expert", None),
            P("expert", "cache", None),
            P("expert", "cache", None),
            P("expert"),
            P("cache", None),
            P(),
            P("cache", "expert", None),
            P("cache", "expert", None),
            P("cache", None, "expert"),
            P(None, "expert", None),
            P(None, "expert", None),
        ),
        out_specs=(
            P(None, "expert", None),
            P("expert", None, "cache"),
            P("expert", None, "cache"),
            P("expert", "cache", None),
        ),
        check_vma=False,
    )
```

time: 228 us -> 192 us (0.84)
  Pallas kernels: 117 us -> 187 us
  starting transfers between devices: 55 us -> 0 us
  blocking collectives: 19.9 us -> 0 us
  local copies, waits for them, and re-layouts: 16.7 us -> 1.31 us
  matrix products: 13.4 us -> 0 us
  other arithmetic: 4.19 us -> 0 us
    pallas_call x1 -> x2, Pallas kernels: 117 us -> 187 us  [the longest x1 184 us: whole_shards(): pl.pallas_call(functools.partial(whole_kernel, C, E, I, S, R, cap), out_s...]
    all_to_all x2 -> x0, starting transfers between devices: 55 us -> none  [the longest x1 49.1 us: shards(): lax.all_to_all(expert_out, 'expert', split_axis=0, concat_axis=0, tiled=T...]
    all_gather x3 -> x0, blocking collectives: 19.9 us -> none  [the longest x1 7.3 us: shards(): lax.all_gather(jnp.concatenate((accum, highest, mass), axis=-1), 'cache')]
    dot_general x8 -> x0, matrix products: 13.4 us -> none  [the longest x1 3.32 us: shards(): jnp.einsum('rnk,rpk->rnp', spread, k_cache, preferred_element_type=jnp.fl...]
    unnamed x11 -> x0, local copies, waits for them, and re-layouts: 11.4 us -> none
    reduce_sum x8 -> x0, other arithmetic: 2.55 us -> none  [the longest x1 1.59 us: shards(): mass = jnp.sum(weights, axis=-1)]
  transfers between devices with their start and end apart: 2 -> 0, of which waited for: 0 -> 0; matrix products, arithmetic and copies ran while one was open for 4% -> 0% of each run, Pallas kernels for 52% -> 0%
where the time goes in v1:
time: 192 us; the launch traced here: 189 us
  Pallas kernels  187 us (97%)
    pallas_call x1, Pallas kernels, whole_shards(): pl.pallas_call(functools.partial(whole_kernel, C, E, I, S, R, cap), out_s...  184 us

profile of v1, /device:TPU:0, one launch (start us, length us, event | category | flops | bytes accessed | tf_op | source)
XLA Modules:
  0.0 189.2 jit_solution(18380024808609058960)
XLA Ops:
  0.6 1.3 reshape.23.gain_ref
  1.9 183.9 %shard_map.138 = (bf16[360,2880]{1,0:T(8,128)(2,1)S(1)}, bf16[360,2880]{1,0:T(8,128)(2,1)S(1)}, bf16[360,2880]{1,0:T(8,128)(2,1)S(1)}, f32[8,2880]{1,0:T(8,128)S(1)}) custom-call(s32[4]{0:T(128)} %lengths.1, s32[2,4,4]{2,1,0:T(4,128)} %ids.1, f32[2,4,4]{2,1,0:T(4,128)} %gates.1, bf16[2,4,2048]{2,1,0:T(4,128)(2,1)} %q_ref.1, f32[1,2880]{1,0:T(1,128)} %reshape.23.gain_ref, ...), custom_call_target="tpu_custom_call" | custom-call | tf_op jit(solution)/shard_map/pallas_call | solution.py:477
  185.9 3.4 %shard_map.139 = (bf16[360,2880]{1,0:T(8,128)(2,1)}, bf16[360,2880]{1,0:T(8,128)(2,1)}, bf16[360,2880]{1,0:T(8,128)(2,1)}, bf16[2,4,2880]{2,1,0:T(4,128)(2,1)}) custom-call(bf16[360,2880]{1,0:T(8,128)(2,1)S(1)} %get-tuple-element.12.g_ref, bf16[360,2880]{1,0:T(8,128)(2,1)S(1)} %get-tuple-element.13.u_ref, bf16[360,2880]{1,0:T(8,128)(2,1)S(1)} %get-tuple-element.14.d_ref, ...), custom_call_target="tpu_custom_call" | custom-call | tf_op jit(solution)/shard_map/pallas_call | solution.py:556

commit v2 on v1

--- a/solution.py
+++ b/solution.py
@@ -36,8 +36,8 @@
     C, E, I, S, R, cap,
     lengths, ids, gates, q_ref, gain_ref, k_hbm, v_hbm, wo_hbm, wg_hbm, wu_hbm, wd_hbm,
     g_own, u_own, d_own, mixed_ref,
-    g_in, u_in, d_in, g_stage, u_stage, relay_g, relay_u, relay_d, fin_g, fin_u, fin_d,
-    k_in, v_in, wo_in, q_f32, part_out, part_in, proj, normed, out_slots, in_slots, slots_bf, slots_all,
+    g_in, u_in, d_in, g_stage, u_stage, d_stage, relay_g, relay_u, relay_d, fin_g, fin_u, fin_d,
+    k_in, v_in, wo_in, q_f32, part_out, part_in, proj, normed, out_slots, slots_all,
     rows_x, hid_out, hid_in, back_out, back_in, comb,
     load_sem, sx, r1, sd, sr, rf, loc, s_part, r_part, s_proj, r_proj, s_disp, r_disp, s_slot, r_slot,
     s_hid, r_hid, s_back, r_back, s_comb, r_comb,
@@ -48,36 +48,33 @@
     k = lax.rem(c, NEAR)
     O = C - NEAR
     width = g_own.shape[0]
-    rows = fin_g.shape[2]
+    rows = g_in.shape[1]
+    full = rows // 128 * 128
+    rest = rows - full
     group = QH // KVH
     per_row = group * S
     heads_rows = KVH * per_row
     items = S * cap
     total = S * R
-    chunk = out_slots.shape[1] * 2
-    half = chunk // 2
+    half = out_slots.shape[2]
+    chunk = half * 2
     d_model = E * rows
 
-    loads = []
-    for i in range(I):
-        loads.append(pltpu.make_async_copy(wg_hbm.at[i], g_in.at[i], load_sem.at[0, i]))
-    loads.append(pltpu.make_async_copy(k_hbm, k_in, load_sem.at[3, 0]))
-    loads.append(pltpu.make_async_copy(v_hbm, v_in, load_sem.at[3, 1]))
-    for i in range(I):
-        loads.append(pltpu.make_async_copy(wu_hbm.at[i], u_in.at[i], load_sem.at[1, i]))
-    loads.append(pltpu.make_async_copy(wd_hbm, d_in, load_sem.at[2, 0]))
-    loads.append(pltpu.make_async_copy(wo_hbm, wo_in, load_sem.at[2, 1]))
+    load_k = pltpu.make_async_copy(k_hbm, k_in, load_sem.at[3, 0])
+    load_v = pltpu.make_async_copy(v_hbm, v_in, load_sem.at[3, 1])
+    load_g = [pltpu.make_async_copy(wg_hbm.at[i], g_in.at[i], load_sem.at[0, i]) for i in range(I)]
+    load_u = [pltpu.make_async_copy(wu_hbm.at[i], u_in.at[i], load_sem.at[1, i]) for i in range(I)]
+    load_d = pltpu.make_async_copy(wd_hbm, d_in, load_sem.at[2, 0])
+    load_wo = pltpu.make_async_copy(wo_hbm, wo_in, load_sem.at[2, 1])
+    loads = [load_k, load_v, load_g[0], load_wo] + load_g[1:] + load_u + [load_d]
     for load in loads:
         load.start()
-    load_g, load_k, load_v = loads[:I], loads[I], loads[I + 1]
-    load_u, load_d, load_wo = loads[I + 2 : 2 * I + 2], loads[2 * I + 2], loads[2 * I + 3]
 
     barrier = pltpu.get_barrier_semaphore()
     me = c * E + e
     for n in range(1, C * E):
         other = lax.rem(me + n, C * E)
         pl.semaphore_signal(barrier, inc=1, device_id=(other // E, lax.rem(other, E)), device_id_type=MESH)
-    pl.semaphore_wait(barrier, C * E - 1)
 
     relays = (relay_g, relay_u, relay_d)
     finals = (fin_g, fin_u, fin_d)
@@ -88,7 +85,7 @@
         )
 
     def block(w, i, target):
-        return (g_stage, u_stage, d_in)[w].at[i, target]
+        return (g_stage, u_stage, d_stage)[w].at[i, target]
 
     def far(o):
         return lax.rem(x * NEAR + NEAR + o, C)
@@ -147,24 +144,43 @@
         def _():
             remote(finals[w].at[s], finals[w].at[s], sd.at[w, 0, 0], rf.at[w, s], c, s).wait_recv()
 
+    tiles = -(-width // 128)
+
     def stage(w, i):
-        source, target = (g_in, u_in)[w], (g_stage, u_stage)[w]
         for t in range(C):
-            target[i, t] = source[i, :, t * width : (t + 1) * width].T
+            if w < 2:
+                part = (g_in, u_in)[w][i, :, t * width : (t + 1) * width]
+                main, last = part[:full].T, part[full:]
+            else:
+                main, last = d_in[i, t, :, :full], d_in[i, t, :, full:].T
+            target = (g_stage, u_stage, d_stage)[w]
+            for j in range(full // 128):
+                target[i, t, j * width : (j + 1) * width, :] = main[:, j * 128 : (j + 1) * 128]
+            last = jnp.concatenate([last, jnp.zeros((rest, tiles * 128 - width), BF16)], axis=1)
+            base = full // 128 * width
+            for j in range(tiles):
+                target[i, t, base + j * rest : base + (j + 1) * rest, :] = last[:, j * 128 : (j + 1) * 128]
 
     def put_together(w):
         own = (g_own, u_own, d_own)[w]
         for s in range(E):
             arrived(w, s)
-            own[:, s * rows : (s + 1) * rows] = finals[w][s]
-
-    for i in range(I):
-        load_g[i].wait()
-        stage(0, i)
-        for o in range(O):
-            hop(0, i, o, "start")
-        for kd in range(NEAR):
-            direct(0, i, kd, "start")
+            for j in range(full // 128):
+                at = s * rows + j * 128
+                own[:, at : at + 128] = finals[w][s, j * width : (j + 1) * width, :]
+            base = full // 128 * width
+            last = jnp.concatenate(
+                [finals[w][s, base + j * rest : base + (j + 1) * rest, :] for j in range(tiles)], axis=1
+            )
+            own[:, s * rows + full : (s + 1) * rows] = last[:, :width].T
+
+    def gather_cache(buffer, send, recv, n, action):
+        target = lax.rem(c + n, C)
+        if action == "recv":
+            remote(buffer.at[target], buffer.at[target], send.at[target], recv.at[target], target, e).wait_recv()
+            return
+        copy = remote(buffer.at[c], buffer.at[c], send.at[target], recv.at[c], target, e)
+        copy.start() if action == "start" else copy.wait_send()
 
     for s in range(S):
         q_f32[s * R : (s + 1) * R, :] = q_ref[s].astype(F32)
@@ -204,6 +220,8 @@
             piece = jnp.where(lane_t < HD, piece, jnp.where(lane_t < HD + 32, highest[span], mass[span]))
             part_out[h, r * per_row : (r + 1) * per_row, :] = piece
 
+    pl.semaphore_wait(barrier, C * E - 1)
+
     def part(n, action):
         target = lax.rem(c + n, C)
         if action == "recv":
@@ -216,40 +234,23 @@
         part(n, "start")
     part_in[c] = part_out[c]
 
-    for i in range(I):
-        load_u[i].wait()
-        stage(1, i)
+    def leave(w, i):
+        if w < 2:
+            (load_g, load_u)[w][i].wait()
+        stage(w, i)
         for o in range(O):
-            hop(1, i, o, "start")
+            hop(w, i, o, "start")
+
+    def straight(w, i):
+        for kd in range(NEAR):
+            direct(w, i, kd, "start")
+
+    def onward(w, i):
         for o in range(O):
-            pass_on(0, o, i, "start")
-        for kd in range(NEAR):
-            direct(1, i, kd, "start")
-
-    def table(shape, row_axis):
-        row = iota(shape, row_axis)
-        slot = iota(shape, 1 - row_axis)
-        expert = slot // (2 * items)
-        inside = lax.rem(slot, items)
-        chosen = jnp.zeros(shape, F32)
-        weight = jnp.zeros(shape, F32)
-        for s in range(S):
-            for r in range(R):
-                for t in range(TOP):
-                    hit = (row == s * R + r) & (expert == ids[s, r, t])
-                    chosen = jnp.where(hit, 1.0, chosen)
-                    weight = jnp.where(hit, gates[s, r, t], weight)
-        rank = jnp.zeros(shape, F32)
-        place = lax.rem(row, R)
-        for n in range(1, R):
-            rank = rank + jnp.where(place >= n, pltpu.roll(chosen, n, row_axis), 0.0)
-        fit = (row < total) & (inside // cap == row // R) & (rank == lax.rem(inside, cap).astype(F32))
-        chosen = jnp.where(fit, chosen, 0.0)
-        return chosen, weight * chosen
-
-    send_table, _ = table((E * 2 * items, 128), 1)
-    _, gate_table = table((total, 128), 0)
-
+            pass_on(w, o, i, "start")
+
+    leave(0, 0)
+    straight(0, 0)
     for n in range(1, C):
         part(n, "recv")
     tall = R * per_row
@@ -277,24 +278,37 @@
     load_wo.wait()
     proj[c] = dot_nt(heads_out, wo_in[...])
 
-    def gather_cache(buffer, send, recv, n, action):
-        target = lax.rem(c + n, C)
-        if action == "recv":
-            remote(buffer.at[target], buffer.at[target], send.at[target], recv.at[target], target, e).wait_recv()
-            return
-        copy = remote(buffer.at[c], buffer.at[c], send.at[target], recv.at[c], target, e)
-        copy.start() if action == "start" else copy.wait_send()
-
     for n in range(1, C):
         gather_cache(proj, s_proj, r_proj, n, "start")
 
-    load_d.wait()
-    for i in range(I):
-        for o in range(O):
-            hop(2, i, o, "start")
-    for i in range(I):
-        for o in range(O):
-            pass_on(1, o, i, "start")
+    leave(0, 1)
+    straight(0, 1)
+    leave(1, 0)
+    def table(shape, row_axis):
+        row = iota(shape, row_axis)
+        slot = iota(shape, 1 - row_axis)
+        expert = slot // (2 * items)
+        inside = lax.rem(slot, items)
+        chosen = jnp.zeros(shape, F32)
+        weight = jnp.zeros(shape, F32)
+        for s in range(S):
+            for r in range(R):
+                for t in range(TOP):
+                    hit = (row == s * R + r) & (expert == ids[s, r, t])
+                    chosen = jnp.where(hit, 1.0, chosen)
+                    weight = jnp.where(hit, gates[s, r, t], weight)
+        rank = jnp.zeros(shape, F32)
+        place = lax.rem(row, R)
+        for n in range(1, R):
+            rank = rank + jnp.where(place >= n, pltpu.roll(chosen, n, row_axis), 0.0)
+        fit = (row < total) & (inside // cap == row // R) & (rank == lax.rem(inside, cap).astype(F32))
+        chosen = jnp.where(fit, chosen, 0.0)
+        return chosen, weight * chosen
+
+    send_table, _ = table((E * 2 * items, 128), 1)
+    _, gate_table = table((total, 128), 0)
+
+    onward(0, 0)
     for n in range(1, C):
         gather_cache(proj, s_proj, r_proj, n, "recv")
     attention = proj[0]
@@ -302,50 +316,52 @@
         attention = attention + proj[s]
     scale = lax.rsqrt(jnp.sum(attention * attention, axis=1, keepdims=True) * (1.0 / d_model) + 1e-05)
     normed[:, d_model:] = jnp.zeros((total, C * chunk - d_model), F32)
-    normed[:, :d_model] = (attention * scale * gain_ref[...]).astype(BF16).astype(F32)
+    normed[:, :d_model] = (attention * scale * gain_ref[...].reshape(1, d_model)).astype(BF16).astype(F32)
     own_chunk = normed[:, pl.ds(pl.multiple_of(c * chunk, 128), chunk)]
     placed = dot_nn(send_table[:, :total], own_chunk)
     upper = lax.rem(iota((E * 2 * items, half), 0), 2 * items) < items
-    out_slots[...] = jnp.where(upper, placed[:, :half], placed[:, half:])
-    step8 = 2 * items
-
-    def at_expert(buffer, index):
-        return buffer.at[pl.ds(pl.multiple_of(index * step8, step8), step8)]
+    out_slots[...] = jnp.where(upper, placed[:, :half], placed[:, half:]).reshape(out_slots.shape).astype(BF16)
 
     def spread_expert(out, back, send, recv, n, action):
         target = lax.rem(e + n, E)
         if action == "recv":
-            spot = at_expert(back, target)
+            spot = back.at[target]
             remote(spot, spot, send.at[target], recv.at[target], c, target).wait_recv()
             return
-        copy = remote(at_expert(out, target), at_expert(back, e), send.at[target], recv.at[e], c, target)
+        copy = remote(out.at[target], back.at[e], send.at[target], recv.at[e], c, target)
         copy.start() if action == "start" else copy.wait_send()
 
     for n in range(1, E):
-        spread_expert(out_slots, in_slots, s_disp, r_disp, n, "start")
-    in_slots[pl.ds(pl.multiple_of(e * step8, step8), step8), :] = out_slots[pl.ds(pl.multiple_of(e * step8, step8), step8), :]
-
-    direct(2, 0, 0, "start")
-    direct(2, 0, 1, "start")
-    for i in range(I):
-        for o in range(O):
-            pass_on(2, o, i, "start")
+        spread_expert(out_slots, slots_all.at[c], s_disp, r_disp, n, "start")
+    slots_all[c, e] = out_slots[e]
+
+    straight(1, 0)
+    onward(0, 1)
+    leave(1, 1)
+    load_d.wait()
+    leave(2, 0)
+    leave(2, 1)
+    onward(1, 0)
+    straight(1, 1)
+    onward(1, 1)
     for n in range(1, E):
-        spread_expert(out_slots, in_slots, s_disp, r_disp, n, "recv")
-    slots_all[c] = in_slots[...].astype(BF16)
+        spread_expert(out_slots, slots_all.at[c], s_disp, r_disp, n, "recv")
     for n in range(1, C):
         gather_cache(slots_all, s_slot, r_slot, n, "start")
+    straight(2, 0)
+    onward(2, 0)
     for n in range(1, C):
         gather_cache(slots_all, s_slot, r_slot, n, "recv")
     count = E * items
     row_t = iota((count, 2 * count), 0)
     col_t = iota((count, 2 * count), 1)
-    base = (row_t // items) * step8 + lax.rem(row_t, items)
+    base = (row_t // items) * (2 * items) + lax.rem(row_t, items)
     take_low = (col_t == base).astype(F32).astype(BF16)
     take_high = (col_t == base + items).astype(F32).astype(BF16)
     for s in range(C):
-        rows_x[:, s * chunk : s * chunk + half] = dot_nn(take_low, slots_all[s]).astype(BF16)
-        rows_x[:, s * chunk + half : (s + 1) * chunk] = dot_nn(take_high, slots_all[s]).astype(BF16)
+        slots = slots_all[s].astype(F32).reshape(2 * count, half).astype(BF16)
+        rows_x[:, s * chunk : s * chunk + half] = dot_nn(take_low, slots).astype(BF16)
+        rows_x[:, s * chunk + half : (s + 1) * chunk] = dot_nn(take_high, slots).astype(BF16)
 
     put_together(0)
     gate_value = dot_nt(rows_x[:, :d_model], g_own[...])
@@ -373,9 +389,8 @@
 
     for n in range(E):
         hidden(n, "start")
-    for i in range(1, I):
-        for kd in range(NEAR):
-            direct(2, i, kd, "start")
+    direct(2, 1, 0, "start")
+    pass_on(2, 0, 1, "start")
     down = []
     for i in range(I):
         value = jnp.zeros((count, rows), F32)
@@ -393,21 +408,23 @@
             lax.rem(row_b, I * items) // items == i
         )
         back = back + dot_nn(pick.astype(F32).astype(BF16), down[i])
-    back_out[...] = back
+    back_out[...] = back.reshape(back_out.shape).astype(BF16)
     for n in range(1, E):
         spread_expert(back_out, back_in, s_back, r_back, n, "start")
-    back_in[pl.ds(pl.multiple_of(e * step8, step8), step8), :] = back_out[pl.ds(pl.multiple_of(e * step8, step8), step8), :]
+    direct(2, 1, 1, "start")
+    pass_on(2, 1, 1, "start")
+    back_in[e] = back_out[e]
     turned = pltpu.roll(gate_table, lax.rem(128 - c * (I * 2 * items), 128), 1)
     for n in range(1, E):
         spread_expert(back_out, back_in, s_back, r_back, n, "recv")
     for s in range(E):
         value = jnp.zeros((total, rows), F32)
+        given = back_in[s].astype(F32)
         for i in range(I):
             for j in range(items):
-                line = back_in[s * step8 + i * items + j : s * step8 + i * items + j + 1, :]
                 lane = i * 2 * items + j
-                value = value + turned[:, lane : lane + 1] * line
-        comb[c, s] = value
+                value = value + turned[:, lane : lane + 1] * given[i * items + j : i * items + j + 1, :]
+        comb[c, s] = value.astype(BF16)
     for n in range(1, C):
         gather_cache(comb, s_comb, r_comb, n, "start")
     put_together(2)
@@ -415,9 +432,9 @@
         gather_cache(comb, s_comb, r_comb, n, "recv")
     pieces = []
     for s in range(E):
-        value = comb[0, s]
+        value = comb[0, s].astype(F32)
         for m in range(1, C):
-            value = value + comb[m, s]
+            value = value + comb[m, s].astype(F32)
         pieces.append(value)
     mixed_ref[...] = attention + jnp.concatenate(pieces, axis=1)
 
@@ -434,7 +451,7 @@
         gather_cache(slots_all, s_slot, r_slot, n, "send")
         gather_cache(comb, s_comb, r_comb, n, "send")
     for n in range(1, E):
-        spread_expert(out_slots, in_slots, s_disp, r_disp, n, "send")
+        spread_expert(out_slots, slots_all.at[c], s_disp, r_disp, n, "send")
         spread_expert(back_out, back_in, s_back, r_back, n, "send")
     for n in range(E):
         hidden(n, "send")
@@ -474,6 +491,7 @@
     V = pltpu.VMEM
     sem = pltpu.SemaphoreType.DMA
     per_row = QH // KVH * S
+    lines = rows // 128 * width + -(-width // 128) * (rows % 128)
     gate, up, down, mixed = pl.pallas_call(
         functools.partial(whole_kernel, C, E, I, S, R, cap),
         out_shape=(
@@ -488,14 +506,15 @@
             V((I, rows, hidden_width), BF16),
             V((I, rows, hidden_width), BF16),
             V((I, C, width, rows), BF16),
-            V((I, C, width, rows), BF16),
-            V((I, C, width, rows), BF16),
-            V((O, I, width, rows), BF16),
-            V((O, I, width, rows), BF16),
-            V((O, I, width, rows), BF16),
-            V((E, width, rows), BF16),
-            V((E, width, rows), BF16),
-            V((E, width, rows), BF16),
+            V((I, C, lines, 128), BF16),
+            V((I, C, lines, 128), BF16),
+            V((I, C, lines, 128), BF16),
+            V((O, I, lines, 128), BF16),
+            V((O, I, lines, 128), BF16),
+            V((O, I, lines, 128), BF16),
+            V((E, lines, 128), BF16),
+            V((E, lines, 128), BF16),
+            V((E, lines, 128), BF16),
             V(k_cache.shape, BF16),
             V(v_cache.shape, BF16),
             V((d_model, w_out.shape[0]), BF16),
@@ -504,16 +523,14 @@
             V((C, R * per_row, 128), F32),
             V((C, S * R, d_model), F32),
             V((S * R, C * chunk), F32),
-            V((E * 2 * items, chunk // 2), F32),
-            V((E * 2 * items, chunk // 2), F32),
-            V((8, 128), BF16),
-            V((C, E * 2 * items, chunk // 2), BF16),
+            V((E, 2 * items, chunk // 2), BF16),
+            V((C, E, 2 * items, chunk // 2), BF16),
             V((E * items, C * chunk), BF16),
             V((E * items, width), BF16),
             V((I, C, E * items, width), BF16),
-            V((I * E * items, rows), F32),
-            V((I * E * items, rows), F32),
-            V((C, E, S * R, rows), F32),
+            V((E, I * items, rows), BF16),
+            V((E, I * items, rows), BF16),
+            V((C, E, S * R, rows), BF16),
             sem((4, 2)),
             sem((3, I, O)),
             sem((3, O, I)),
@@ -544,7 +561,7 @@
         expert_ids,
         gate_weights,
         queries,
-        norm_gain.reshape(1, d_model),
+        norm_gain,
         k_cache,
         v_cache,
         w_out.T,
@@ -713,6 +730,8 @@
         and C == KVH
         and I * C == E
         and rows % 8 == 0
+        and rows % 128 > 0
+        and rows > 128
         and hidden_width % (8 * C) == 0
         and w_out.shape[0] * C == QH * HD
         and queries.shape[0] * queries.shape[1] == 8

time: 192 us -> 173 us (0.901)
  Pallas kernels: 187 us -> 170 us
    pallas_call x1, Pallas kernels: 184 us -> 166 us  [whole_shards(): pl.pallas_call(functools.partial(whole_kernel, C, E, I, S, R, cap), out_s...]
where the time goes in v2:
time: 173 us; the launch traced here: 170 us
  Pallas kernels  170 us (98%)
    pallas_call x1, Pallas kernels, whole_shards(): pl.pallas_call(functools.partial(whole_kernel, C, E, I, S, R, cap), out_s...  166 us

profile of v2, /device:TPU:0, one launch (start us, length us, event | category | flops | bytes accessed | tf_op | source)
XLA Modules:
  0.0 170.4 jit_solution(1619472808886263949)
XLA Ops:
  0.6 166.3 %shard_map.138 = (bf16[360,2880]{1,0:T(8,128)(2,1)S(1)}, bf16[360,2880]{1,0:T(8,128)(2,1)S(1)}, bf16[360,2880]{1,0:T(8,128)(2,1)S(1)}, f32[8,2880]{1,0:T(8,128)S(1)}) custom-call(s32[4]{0:T(128)} %lengths.1, s32[2,4,4]{2,1,0:T(4,128)} %ids.1, f32[2,4,4]{2,1,0:T(4,128)} %gates.1, bf16[2,4,2048]{2,1,0:T(4,128)(2,1)} %q_ref.1, f32[2880]{0:T(1024)} %gain_ref.1, ...), custom_call_target="tpu_custom_call" | custom-call | tf_op jit(solution)/shard_map/pallas_call | solution.py:495
  167.0 3.4 %shard_map.139 = (bf16[360,2880]{1,0:T(8,128)(2,1)}, bf16[360,2880]{1,0:T(8,128)(2,1)}, bf16[360,2880]{1,0:T(8,128)(2,1)}, bf16[2,4,2880]{2,1,0:T(4,128)(2,1)}) custom-call(bf16[360,2880]{1,0:T(8,128)(2,1)S(1)} %get-tuple-element.12.g_ref, bf16[360,2880]{1,0:T(8,128)(2,1)S(1)} %get-tuple-element.13.u_ref, bf16[360,2880]{1,0:T(8,128)(2,1)S(1)} %get-tuple-element.14.d_ref, ...), custom_call_target="tpu_custom_call" | custom-call | tf_op jit(solution)/shard_map/pallas_call | solution.py:573

commit v3 on v2

--- a/solution.py
+++ b/solution.py
@@ -34,12 +34,12 @@
 
 def whole_kernel(
     C, E, I, S, R, cap,
-    lengths, ids, gates, q_ref, gain_ref, k_hbm, v_hbm, wo_hbm, wg_hbm, wu_hbm, wd_hbm,
+    lengths, ids, gates, q_hbm, gain_hbm, k_hbm, v_hbm, wo_hbm, wg_hbm, wu_hbm, wd_hbm,
     g_own, u_own, d_own, mixed_ref,
     g_in, u_in, d_in, g_stage, u_stage, d_stage, relay_g, relay_u, relay_d, fin_g, fin_u, fin_d,
-    k_in, v_in, wo_in, q_f32, part_out, part_in, proj, normed, out_slots, slots_all,
+    k_in, v_in, wo_in, q_ref, gain_ref, q_f32, part_out, part_in, proj, normed, out_slots, slots_all,
     rows_x, hid_out, hid_in, back_out, back_in, comb,
-    load_sem, sx, r1, sd, sr, rf, loc, s_part, r_part, s_proj, r_proj, s_disp, r_disp, s_slot, r_slot,
+    load_sem, row_sem, sx, r1, r2, sd, sr, rf, loc, s_part, r_part, s_proj, r_proj, s_disp, r_disp, s_slot, r_slot,
     s_hid, r_hid, s_back, r_back, s_comb, r_comb,
 ):
     c = lax.axis_index("cache")
@@ -60,13 +60,15 @@
     chunk = half * 2
     d_model = E * rows
 
-    load_k = pltpu.make_async_copy(k_hbm, k_in, load_sem.at[3, 0])
-    load_v = pltpu.make_async_copy(v_hbm, v_in, load_sem.at[3, 1])
+    load_q = pltpu.make_async_copy(q_hbm, q_ref, load_sem.at[3, 0])
+    load_gain = pltpu.make_async_copy(gain_hbm, gain_ref, load_sem.at[3, 1])
+    load_k = [pltpu.make_async_copy(k_hbm.at[r], k_in.at[r], row_sem.at[0, r]) for r in range(R)]
+    load_v = [pltpu.make_async_copy(v_hbm.at[r], v_in.at[r], row_sem.at[1, r]) for r in range(R)]
     load_g = [pltpu.make_async_copy(wg_hbm.at[i], g_in.at[i], load_sem.at[0, i]) for i in range(I)]
     load_u = [pltpu.make_async_copy(wu_hbm.at[i], u_in.at[i], load_sem.at[1, i]) for i in range(I)]
     load_d = pltpu.make_async_copy(wd_hbm, d_in, load_sem.at[2, 0])
     load_wo = pltpu.make_async_copy(wo_hbm, wo_in, load_sem.at[2, 1])
-    loads = [load_k, load_v, load_g[0], load_wo] + load_g[1:] + load_u + [load_d]
+    loads = [load_q] + [load for pair in zip(load_k, load_v) for load in pair] + [load_g[0], load_wo, load_gain] + load_g[1:] + load_u + [load_d]
     for load in loads:
         load.start()
 
@@ -87,6 +89,9 @@
     def block(w, i, target):
         return (g_stage, u_stage, d_stage)[w].at[i, target]
 
+    lines = g_stage.shape[2]
+    parts = (pl.ds(0, lines // 16 * 8), pl.ds(lines // 16 * 8, lines - lines // 16 * 8))
+
     def far(o):
         return lax.rem(x * NEAR + NEAR + o, C)
 
@@ -105,6 +110,21 @@
             copy = remote(block(w, i, target), finals[w].at[e], sd.at[w, i, kd], rf.at[w, e], target, owner)
             copy.start() if action == "start" else copy.wait_send()
 
+    last = (2, I - 1, O - 1)
+
+    def around(source):
+        here = e // I
+        crossing = (here < C // 2) != (source < C // 2)
+        return crossing & (jnp.abs(here - source) == 1)
+
+    def send_around():
+        w, i, o = last
+        target = far(o)
+
+        @pl.when(around(c))
+        def _():
+            remote(block(w, i, target), finals[w].at[e], sx.at[w, i, o], rf.at[w, e], target, c * I + i).start()
+
     def hop(w, i, o, action):
         target = far(o)
         owner = c * I + i
@@ -115,23 +135,41 @@
             copy = remote(block(w, i, target), finals[w].at[e], sx.at[w, i, o], rf.at[w, e], target, e)
             copy.start() if action == "start" else copy.wait_send()
 
-        @pl.when(owner != e)
+        away = owner != e
+        if action == "start" and (w, i, o) == last:
+            away = away & jnp.logical_not(around(c))
+
+        @pl.when(away)
         def _():
-            copy = remote(block(w, i, target), relays[w].at[place, i], sx.at[w, i, o], r1.at[w, place, i], target, e)
-            copy.start() if action == "start" else copy.wait_send()
+            if action == "send" or (w, i) != (0, 0):
+                copy = remote(block(w, i, target), relays[w].at[place, i], sx.at[w, i, o], r1.at[w, place, i], target, e)
+                copy.start() if action == "start" else copy.wait_send()
+            else:
+                for part, arrival in zip(parts, (r1.at[w, place, i], r2.at[place])):
+                    remote(
+                        block(w, i, target).at[part], relays[w].at[place, i, part], sx.at[w, i, o], arrival, target, e
+                    ).start()
 
     def pass_on(w, o, i, action):
         owner = far(o) * I + i
 
-        @pl.when(owner != e)
+        away = owner != e
+        if (w, i) == last[:2]:
+            away = away & jnp.logical_not(around(far(o)) & (k == NEAR - 1))
+
+        @pl.when(away)
         def _():
             part = relays[w].at[o, i]
-            copy = remote(part, finals[w].at[e], sr.at[w, o, i], rf.at[w, e], c, owner)
-            if action == "start":
+            if action == "start" and (w, i) == (0, 0):
+                for span, arrival in zip(parts, (r1.at[w, o, i], r2.at[o])):
+                    half = relays[w].at[o, i, span]
+                    remote(half, half, sr.at[w, o, i], arrival, c, owner).wait_recv()
+                    remote(half, finals[w].at[e, span], sr.at[w, o, i], rf.at[w, e], c, owner).start()
+            elif action == "start":
                 remote(part, part, sr.at[w, o, i], r1.at[w, o, i], c, owner).wait_recv()
-                copy.start()
+                remote(part, finals[w].at[e], sr.at[w, o, i], rf.at[w, e], c, owner).start()
             else:
-                copy.wait_send()
+                remote(part, finals[w].at[e], sr.at[w, o, i], rf.at[w, e], c, owner).wait_send()
 
     def arrived(w, s):
         own = (c == e // I) & (e == s)
@@ -182,8 +220,6 @@
         copy = remote(buffer.at[c], buffer.at[c], send.at[target], recv.at[c], target, e)
         copy.start() if action == "start" else copy.wait_send()
 
-    for s in range(S):
-        q_f32[s * R : (s + 1) * R, :] = q_ref[s].astype(F32)
     lane_q = iota((heads_rows, QH * HD), 1)
     row_q = iota((heads_rows, QH * HD), 0)
     head_of_row = (row_q // per_row) * group + lax.rem(row_q, per_row) // S
@@ -192,8 +228,9 @@
     fold_l = iota((QH * HD, KVH * HD), 0)
     fold_m = iota((QH * HD, KVH * HD), 1)
     fold = ((lax.rem(fold_l, HD) == lax.rem(fold_m, HD)) & (fold_l // (group * HD) == fold_m // HD)).astype(F32).astype(BF16)
-    load_k.wait()
-    load_v.wait()
+    load_q.wait()
+    for s in range(S):
+        q_f32[s * R : (s + 1) * R, :] = q_ref[s].astype(F32)
     positions = k_in.shape[1]
     place_of = c * positions + iota((heads_rows, positions), 1)
     step_p = lax.rem(iota((heads_rows, positions), 0), S)
@@ -205,11 +242,13 @@
             spread = jnp.where(step_q == s, jnp.broadcast_to(q_f32[s * R + r : s * R + r + 1, :], spread.shape), spread)
         spread = jnp.where(mine, spread, 0.0).astype(BF16)
         spread = dot_nn(spread, fold).astype(BF16)
+        load_k[r].wait()
         score = dot_nt(spread, k_in[r]) * (1.0 / math.sqrt(HD))
         visible = place_of < lengths[r] + step_p + 1
         highest = jnp.max(jnp.where(visible, score, -1e30), axis=1, keepdims=True)
         weight = jnp.where(visible, jnp.exp(score - highest), 0.0)
         mass = jnp.sum(weight, axis=1, keepdims=True)
+        load_v[r].wait()
         accum = dot_nn(weight.astype(BF16), v_in[r])
         for h in range(KVH):
             span = slice(h * per_row, (h + 1) * per_row)
@@ -315,6 +354,7 @@
     for s in range(1, C):
         attention = attention + proj[s]
     scale = lax.rsqrt(jnp.sum(attention * attention, axis=1, keepdims=True) * (1.0 / d_model) + 1e-05)
+    load_gain.wait()
     normed[:, d_model:] = jnp.zeros((total, C * chunk - d_model), F32)
     normed[:, :d_model] = (attention * scale * gain_ref[...].reshape(1, d_model)).astype(BF16).astype(F32)
     own_chunk = normed[:, pl.ds(pl.multiple_of(c * chunk, 128), chunk)]
@@ -350,6 +390,7 @@
         gather_cache(slots_all, s_slot, r_slot, n, "start")
     straight(2, 0)
     onward(2, 0)
+    direct(2, 1, 0, "start")
     for n in range(1, C):
         gather_cache(slots_all, s_slot, r_slot, n, "recv")
     count = E * items
@@ -389,7 +430,8 @@
 
     for n in range(E):
         hidden(n, "start")
-    direct(2, 1, 0, "start")
+    direct(2, 1, 1, "start")
+    send_around()
     pass_on(2, 0, 1, "start")
     down = []
     for i in range(I):
@@ -411,7 +453,6 @@
     back_out[...] = back.reshape(back_out.shape).astype(BF16)
     for n in range(1, E):
         spread_expert(back_out, back_in, s_back, r_back, n, "start")
-    direct(2, 1, 1, "start")
     pass_on(2, 1, 1, "start")
     back_in[e] = back_out[e]
     turned = pltpu.roll(gate_table, lax.rem(128 - c * (I * 2 * items), 128), 1)
@@ -458,9 +499,11 @@
 
 
 def store_kernel(S, R, g_ref, u_ref, d_ref, mixed_ref, go_hbm, uo_hbm, do_hbm, mo_ref, sems):
+    height = g_ref.shape[0] // 5
     copies = [
-        pltpu.make_async_copy(source, target, sems.at[n])
+        pltpu.make_async_copy(source.at[pl.ds(m * height, height)], target.at[pl.ds(m * height, height)], sems.at[n, m])
         for n, (source, target) in enumerate(((g_ref, go_hbm), (u_ref, uo_hbm), (d_ref, do_hbm)))
+        for m in range(5)
     ]
     for copy in copies:
         copy.start()
@@ -500,7 +543,7 @@
             pltpu.VMEM((width, d_model), BF16),
             pltpu.VMEM((S * R, d_model), F32),
         ),
-        in_specs=[smem, smem, smem, vmem, vmem] + [any_spec] * 6,
+        in_specs=[smem, smem, smem] + [any_spec] * 8,
         out_specs=(vmem,) * 4,
         scratch_shapes=[
             V((I, rows, hidden_width), BF16),
@@ -518,6 +561,8 @@
             V(k_cache.shape, BF16),
             V(v_cache.shape, BF16),
             V((d_model, w_out.shape[0]), BF16),
+            V(queries.shape, BF16),
+            V((d_model,), F32),
             V((S * R, QH * HD), F32),
             V((C, R * per_row, 128), F32),
             V((C, R * per_row, 128), F32),
@@ -532,8 +577,10 @@
             V((E, I * items, rows), BF16),
             V((C, E, S * R, rows), BF16),
             sem((4, 2)),
+            sem((2, R)),
             sem((3, I, O)),
             sem((3, O, I)),
+            sem((O,)),
             sem((3, I, NEAR)),
             sem((3, O, I)),
             sem((3, E)),
@@ -580,7 +627,7 @@
         ),
         in_specs=[vmem] * 4,
         out_specs=(any_spec,) * 3 + (vmem,),
-        scratch_shapes=[sem((3,))],
+        scratch_shapes=[sem((3, 5))],
         compiler_params=pltpu.CompilerParams(vmem_limit_bytes=2 << 20),
     )(gate, up, down, mixed)
     return (
@@ -726,13 +773,13 @@
     I, rows, hidden_width = w_gate.shape
     fits = (
         C % NEAR == 0
-        and C > NEAR
+        and C == 2 * NEAR
         and C == KVH
         and I * C == E
         and rows % 8 == 0
         and rows % 128 > 0
         and rows > 128
-        and hidden_width % (8 * C) == 0
+        and hidden_width % (40 * C) == 0
         and w_out.shape[0] * C == QH * HD
         and queries.shape[0] * queries.shape[1] == 8
         and I * queries.shape[0] * 2 == 8

time: 173 us -> 170 us (0.983); the launches traced: 170 us -> 169 us
  no operation moved by 1% of the time
where the time goes in v3:
time: 170 us; the launch traced here: 169 us
  Pallas kernels  169 us (99%)
    pallas_call x1, Pallas kernels, whole_shards(): pl.pallas_call(functools.partial(whole_kernel, C, E, I, S, R, cap), out_s...  165 us
    pallas_call x1, Pallas kernels, whole_shards(): pl.pallas_call(functools.partial(store_kernel, S, R), out_shape=(shape((w...  3.41 us

profile of v3, /device:TPU:0, one launch (start us, length us, event | category | flops | bytes accessed | tf_op | source)
XLA Modules:
  0.0 169.4 jit_solution(15791222549586928621)
XLA Ops:
  0.6 165.2 %shard_map.138 = (bf16[360,2880]{1,0:T(8,128)(2,1)S(1)}, bf16[360,2880]{1,0:T(8,128)(2,1)S(1)}, bf16[360,2880]{1,0:T(8,128)(2,1)S(1)}, f32[8,2880]{1,0:T(8,128)S(1)}) custom-call(s32[4]{0:T(128)} %lengths.1, s32[2,4,4]{2,1,0:T(4,128)} %ids.1, f32[2,4,4]{2,1,0:T(4,128)} %gates.1, bf16[2,4,2048]{2,1,0:T(4,128)(2,1)} %q_hbm.1, f32[2880]{0:T(1024)} %gain_hbm.1, ...), custom_call_target="tpu_custom_call" | custom-call | tf_op jit(solution)/shard_map/pallas_call | solution.py:538
  165.9 3.4 %shard_map.139 = (bf16[360,2880]{1,0:T(8,128)(2,1)}, bf16[360,2880]{1,0:T(8,128)(2,1)}, bf16[360,2880]{1,0:T(8,128)(2,1)}, bf16[2,4,2880]{2,1,0:T(4,128)(2,1)}) custom-call(bf16[360,2880]{1,0:T(8,128)(2,1)S(1)} %get-tuple-element.12.g_ref, bf16[360,2880]{1,0:T(8,128)(2,1)S(1)} %get-tuple-element.13.u_ref, bf16[360,2880]{1,0:T(8,128)(2,1)S(1)} %get-tuple-element.14.d_ref, ...), custom_call_target="tpu_custom_call" | custom-call | tf_op jit(solution)/shard_map/pallas_call | solution.py:620
